TPU v7x, 32 devices: a whole 2x2x4 slice. The times are simulated.
32 devices in a mesh: wide: 16 (over z, x, core), narrow: 2 (over y).
Axes of the slice: x: 2, y: 2, z: 4, core: 2. Of those that a mesh axis runs over, the one named last changes fastest.
Arguments:
- right_side: float32 [3, 256, 32, 128], P(None, 'wide', 'narrow'), may hold values from -8 to 8
- occupancy: int32 [256, 32, 128], P('wide', 'narrow'), may hold values from 0 to 1, as said below
- region: int32 [256, 32, 128], P('wide', 'narrow'), may hold values from 0 to 3
- coarse_inverse: float32 [384, 384], P(('wide', 'narrow')), as said below
Outputs:
- solution_field: float32 [3, 256, 32, 128], P(None, 'wide', 'narrow')
- residual: float32 [3, 256, 32, 128], P(None, 'wide', 'narrow')
Inputs may be any that keep to these rules, and one draw needn't show every extreme that they name: `occupancy`: each subdomain has its own bone fraction between 0.15 and 0.9. `coarse_inverse`: symmetric positive definite.
All inputs are finite; a program needn't handle non-finite values.
Results may differ from a plain program's by a relative error of at most 0.00021.
Values sent between devices are 32-bit elements; how exact they have to be, the bound alone decides.
A program may use at most 64 MiB of HBM per device.

v0:
```python
import functools

import jax
import jax.numpy as jnp
from jax import lax
from jax.experimental import pallas as pl
from jax.experimental.pallas import tpu as pltpu
from jax.sharding import PartitionSpec as P

LANES = 128
SUB = 8
UNROLL = 16
looped = functools.partial(lax.fori_loop, unroll=UNROLL)
MESH = pl.DeviceIdType.MESH
bone_stiff = 1.0
soft_stiff = 0.1


def kernel(nw, nn, r_hbm, occ_hbm, reg_hbm, ci_hbm,
           z0_v, z1_v, r_v, az_v, y_v, sc_v,
            occ_v, reg_v, c_v, k_p, kx, kym, kyp, kzm, kzp, dg, invd,
           z_p, v_p, zy, vy,
           ix_in, iy_send, iy_in, c_in, wx_send, wx_in, wy_send, wy_in,
           row_send, rows, load_sem, hs_send, hs_recv, ag_send, ag_recv):
    X, Y, Z = occ_v.shape
    ncr, NC = c_v.shape
    G = ncr // 3
    ND = nw * nn
    wi = lax.axis_index("wide")
    ni = lax.axis_index("narrow")
    me = wi * nn + ni
    f32 = jnp.float32

    loads = [pltpu.make_async_copy(s, d, load_sem.at[i]) for i, (s, d) in enumerate(
        ((occ_hbm, occ_v), (reg_hbm, reg_v), (r_hbm, r_v), (ci_hbm, c_v)))]
    for l in loads:
        l.start()

    def peer(i):
        t = lax.rem(me + i, ND)
        return (t // nn, lax.rem(t, nn))

    barrier = pltpu.get_barrier_semaphore()

    def greet(i, _):
        pl.semaphore_signal(barrier, inc=1, device_id=peer(i), device_id_type=MESH)
        return 0

    lax.fori_loop(1, ND, greet, 0, unroll=ND <= 64)

    has = (wi > 0, wi < nw - 1, ni > 0, ni < nn - 1)
    to = ((wi - 1, ni), (wi + 1, ni), (wi, ni - 1), (wi, ni + 1))

    for d in range(4):
        @pl.when(jnp.logical_not(has[d]))
        def _():
            c_in[d] = jnp.zeros((ncr, NC), f32)
            for p in range(2):
                if d < 2:
                    wx_in[p, d] = jnp.zeros((3, Y, Z), f32)
                else:
                    wy_in[p, d - 2] = jnp.zeros((3, X, Z), f32)
            if d < 2:
                ix_in[d] = jnp.zeros((2, Y, Z), jnp.int32)
            else:
                iy_in[d - 2] = jnp.zeros((2, X, Z), jnp.int32)

    loads[0].wait()
    loads[1].wait()

    def pack_ints(x, _):
        iy_send[0, 0, pl.ds(x, 1), :] = occ_v[x, 0:1, :]
        iy_send[1, 0, pl.ds(x, 1), :] = occ_v[x, Y - 1:Y, :]
        iy_send[0, 1, pl.ds(x, 1), :] = reg_v[x, 0:1, :]
        iy_send[1, 1, pl.ds(x, 1), :] = reg_v[x, Y - 1:Y, :]
        return 0

    looped(0, X, pack_ints, 0)

    def fold(a):
        return jnp.sum(a.reshape(Y // SUB, SUB, Z), axis=0)

    def zero_acc(n):
        return tuple(jnp.zeros((SUB, Z), f32) for _ in range(n))

    def add_rc(acc, reg, u):
        out = list(acc)
        for g in range(G):
            m = reg == g
            for c in range(3):
                out[g * 3 + c] = acc[g * 3 + c] + fold(jnp.where(m, u[c], 0.0))
        return tuple(out)

    base = (me * ncr) % LANES

    def make_row(p, acc, first):
        a = jnp.concatenate([jnp.sum(b, axis=0, keepdims=True) for b in acc], axis=0)
        col = jnp.sum(a, axis=1, keepdims=True)
        n = len(acc)
        k = lax.broadcasted_iota(jnp.int32, (n, LANES), 0)
        lane = lax.broadcasted_iota(jnp.int32, (n, LANES), 1)
        target = (base + first + k) & (LANES - 1)
        row = jnp.sum(jnp.where(lane == target, col, 0.0), axis=0, keepdims=True)
        row_send[p, 0:1, :] = row
        rows[p, pl.ds(me, 1), :] = row

    def gather_start(p):
        def send(i, _):
            pltpu.make_async_remote_copy(
                src_ref=row_send.at[p, pl.ds(0, 1)], dst_ref=rows.at[p, pl.ds(me, 1)],
                send_sem=ag_send.at[p], recv_sem=ag_recv.at[p],
                device_id=peer(i), device_id_type=MESH).start()
            return 0
        lax.fori_loop(1, ND, send, 0, unroll=ND <= 64)

    def gather_wait(p, sem):
        part = rows.at[p, pl.ds(0, ND - 1)]
        pltpu.make_async_copy(part, part, sem.at[p]).wait()

    def coarse_vector(p):
        tiles = []
        for t in range(NC // LANES):
            lo = (LANES * t) // ncr // SUB * SUB
            hi = min(ND, -(-(-(-(LANES * (t + 1)) // ncr)) // SUB) * SUB)
            d = lax.broadcasted_iota(jnp.int32, (hi - lo, LANES), 0) + lo
            j = lax.broadcasted_iota(jnp.int32, (hi - lo, LANES), 1) + LANES * t
            m = (j >= d * ncr) & (j < d * ncr + ncr)
            tiles.append(jnp.sum(jnp.where(m, rows[p, lo:hi, :], 0.0), axis=0, keepdims=True))
        return tiles

    def total(p, s):
        d = lax.broadcasted_iota(jnp.int32, (ND, LANES), 0)
        lane = lax.broadcasted_iota(jnp.int32, (ND, LANES), 1)
        m = lane == ((d * ncr + ncr + s) & (LANES - 1))
        v = jnp.sum(jnp.where(m, rows[p], 0.0), axis=0, keepdims=True)
        return jnp.sum(v, axis=1, keepdims=True)

    def answers(tiles, ref):
        s = ref[:, 0:LANES] * tiles[0]
        for t in range(1, len(tiles)):
            s = s + ref[:, t * LANES:(t + 1) * LANES] * tiles[t]
        q = jnp.sum(s, axis=1, keepdims=True)
        return [q[i:i + 1, :] for i in range(ncr)]

    def spread(reg, q):
        masks = [reg == g for g in range(G)]
        out = []
        for c in range(3):
            s = jnp.zeros(reg.shape, f32)
            for g in range(G):
                s = jnp.where(masks[g], q[g * 3 + c], s)
            out.append(s)
        return out

    def halo(slot, d, src, dst):
        return pltpu.make_async_remote_copy(
            src_ref=src, dst_ref=dst, send_sem=hs_send.at[slot, d],
            recv_sem=hs_recv.at[slot, d ^ 1], device_id=to[d], device_id_type=MESH)

    def copies(kind, d):
        e = d ^ 1
        if kind == 0:
            if d < 2:
                x = 0 if d == 0 else X - 1
                return [halo(0, d, occ_v.at[x], ix_in.at[e, 0]),
                        halo(1, d, reg_v.at[x], ix_in.at[e, 1])]
            return [halo(0, d, iy_send.at[d - 2, 0], iy_in.at[e - 2, 0]),
                    halo(1, d, iy_send.at[d - 2, 1], iy_in.at[e - 2, 1])]
        if kind == 1:
            return [halo(2, d, c_v, c_in.at[e])]
        p = kind - 2
        if d < 2:
            return [halo(3 + p, d, wx_send.at[p, d], wx_in.at[p, e])]
        return [halo(3 + p, d, wy_send.at[p, d - 2], wy_in.at[p, e - 2])]

    def halo_start(kind):
        for d in range(4):
            @pl.when(has[d])
            def _():
                for c in copies(kind, d):
                    c.start()

    def halo_wait(kind):
        for d in range(4):
            @pl.when(has[d])
            def _():
                for c in copies(kind, d ^ 1):
                    c.wait_recv()

    def halo_done(kind):
        for d in range(4):
            @pl.when(has[d])
            def _():
                for c in copies(kind, d):
                    c.wait_send()

    loads[2].wait()
    acc = looped(0, X, lambda x, a: add_rc(a, reg_v[x], [r_v[c, x] for c in range(3)]),
                        zero_acc(ncr))
    make_row(0, acc, 0)
    loads[3].wait()

    pl.semaphore_wait(barrier, ND - 1)
    halo_start(0)
    gather_start(0)
    halo_start(1)

    def stiff_of(o):
        return soft_stiff + (bone_stiff - soft_stiff) * o.astype(f32)

    def own_k(x, _):
        k_p[x + 1] = stiff_of(occ_v[x])
        return 0

    looped(0, X, own_k, 0)
    halo_wait(0)
    for d in range(2):
        @pl.when(has[d])
        def _():
            k_p[0 if d == 0 else X + 1] = stiff_of(ix_in[d, 0])

        @pl.when(jnp.logical_not(has[d]))
        def _():
            k_p[0 if d == 0 else X + 1] = jnp.zeros((Y, Z), f32)

    row_id = lax.broadcasted_iota(jnp.int32, (Y, Z), 0)
    lane_id = lax.broadcasted_iota(jnp.int32, (Y, Z), 1)
    side_lo = jnp.where(has[2], 1.0, 0.0).astype(f32)
    side_hi = jnp.where(has[3], 1.0, 0.0).astype(f32)

    def yshift(u, lo, hi):
        down = jnp.where(row_id == 0, lo, pltpu.roll(u, 1, 0))
        up = jnp.where(row_id == Y - 1, hi, pltpu.roll(u, Y - 1, 0))
        return down, up

    def save_faces(p, x, w):
        for c in range(3):
            wy_send[p, 0, c, pl.ds(x, 1), :] = w[c][0:1, :]
            wy_send[p, 1, c, pl.ds(x, 1), :] = w[c][Y - 1:Y, :]

    def coefficients(x, _):
        k = k_p[x + 1]
        lo = stiff_of(iy_in[0, 0, pl.ds(x, 1), :]) * side_lo
        hi = stiff_of(iy_in[1, 0, pl.ds(x, 1), :]) * side_hi
        down, up = yshift(k, lo, hi)
        back = jnp.where(lane_id == 0, 0.0, pltpu.roll(k, 1, 1))
        ahead = jnp.where(lane_id == Z - 1, 0.0, pltpu.roll(k, Z - 1, 1))
        xm = 0.5 * (k + k_p[x])
        xp = 0.5 * (k + k_p[x + 2])
        ym = 0.5 * (k + down)
        yp = 0.5 * (k + up)
        zm = 0.5 * (k + back)
        zp = 0.5 * (k + ahead)
        diag = xm + xp + ym + yp + zm + zp + 0.5 * k
        inv = 1.0 / diag
        kx[x] = xm
        kx[x + 1] = xp
        kym[x] = ym
        kyp[x] = yp
        kzm[x] = jnp.where(lane_id == 0, 0.0, zm)
        kzp[x] = jnp.where(lane_id == Z - 1, 0.0, zp)
        dg[x] = diag - 0.25 * k
        invd[x] = inv
        w = [r_v[c, x] * inv for c in range(3)]
        for c in range(3):
            z_p[c, x + 1] = w[c]
        save_faces(0, x, w)
        return 0

    looped(0, X, coefficients, 0)
    for c in range(3):
        wx_send[0, 0, c] = z_p[c, 1]
        wx_send[0, 1, c] = z_p[c, X]
    halo_start(2)

    def edges(p, qs, pad, side):
        for d in range(2):
            s = spread(ix_in[d, 1], qs[d])
            for c in range(3):
                pad[c, 0 if d == 0 else X + 1] = wx_in[p, d, c] + s[c]
        for d in range(2):
            s = spread(iy_in[d, 1], qs[2 + d])
            for c in range(3):
                side[d, c] = wy_in[p, d, c] + s[c]

    def operate(pad, side, x):
        k = k_p[x + 1]
        u = [pad[c, x + 1] for c in range(3)]
        k4 = 0.25 * k * (u[0] + u[1] + u[2])
        out = []
        for c in range(3):
            down, up = yshift(u[c], side[0, c, pl.ds(x, 1), :], side[1, c, pl.ds(x, 1), :])
            a = dg[x] * u[c] + k4
            a = a - (kx[x] * pad[c, x] + kx[x + 1] * pad[c, x + 2])
            a = a - (kym[x] * down + kyp[x] * up)
            a = a - (kzm[x] * pltpu.roll(u[c], 1, 1) + kzp[x] * pltpu.roll(u[c], Z - 1, 1))
            out.append(a)
        return u, out

    gather_wait(0, ag_recv)
    halo_wait(1)
    tiles = coarse_vector(0)
    q = answers(tiles, c_v)
    qs = [answers(tiles, c_in.at[d]) for d in range(4)]

    def add_spread(x, _):
        s = spread(reg_v[x], q)
        for c in range(3):
            z = z_p[c, x + 1] + s[c]
            z_p[c, x + 1] = z
            z0_v[c, x] = z
        return 0

    looped(0, X, add_spread, 0)
    halo_wait(2)
    edges(0, qs, z_p, zy)

    def dots(a, b):
        return fold(a[0] * b[0] + a[1] * b[1] + a[2] * b[2])

    def first(x, carry):
        u, a = operate(z_p, zy, x)
        r = [r_v[c, x] for c in range(3)]
        w = []
        for c in range(3):
            y_v[c, x] = a[c]
            w.append(a[c] * invd[x])
            v_p[c, x + 1] = w[c]
        save_faces(1, x, w)
        acc = add_rc(carry[:ncr], reg_v[x], a)
        return acc + (carry[ncr] + dots(r, u), carry[ncr + 1] + dots(a, u))

    acc = looped(0, X, first, zero_acc(ncr + 2))
    make_row(1, acc, 0)
    gather_start(1)
    for c in range(3):
        wx_send[1, 0, c] = v_p[c, 1]
        wx_send[1, 1, c] = v_p[c, X]
    halo_start(3)
    halo_wait(3)
    gather_wait(1, ag_recv)
    tiles = coarse_vector(1)
    q = answers(tiles, c_v)
    qs = [answers(tiles, c_in.at[d]) for d in range(4)]
    rz0 = total(1, 0)
    alpha0 = rz0 / total(1, 1)

    def add_spread_v(x, _):
        s = spread(reg_v[x], q)
        for c in range(3):
            v_p[c, x + 1] = v_p[c, x + 1] + s[c]
        return 0

    looped(0, X, add_spread_v, 0)
    edges(1, qs, v_p, vy)

    def second(x, carry):
        u, a = operate(v_p, vy, x)
        r, z, az = [], [], []
        for c in range(3):
            y = y_v[c, x]
            r.append(r_v[c, x] - alpha0 * y)
            z.append(z_p[c, x + 1] - alpha0 * u[c])
            az.append(y - alpha0 * a[c])
            r_v[c, x] = r[c]
            z1_v[c, x] = z[c]
            az_v[c, x] = az[c]
        return (carry[0] + dots(r, z), carry[1] + dots(az, z))

    acc = looped(0, X, second, zero_acc(2))
    make_row(2, acc, ncr)
    gather_start(2)
    gather_wait(2, ag_recv)
    rz1 = total(2, 0)
    beta = rz1 / rz0
    alpha1 = rz1 / (total(2, 1) - beta * rz1 / alpha0)
    along = alpha0 + alpha1 * beta
    a1b = alpha1 * beta

    sc_v[0:1, :] = jnp.broadcast_to(along, (1, LANES))
    sc_v[1:2, :] = jnp.broadcast_to(alpha1, (1, LANES))
    sc_v[2:3, :] = jnp.broadcast_to(a1b, (1, LANES))
    for kind in range(4):
        halo_done(kind)
    for p in range(3):
        gather_wait(p, ag_send)


def finish(z0_v, z1_v, r_v, az_v, y_v, sc_v, x_out, res_out, xb, rb, sem):
    along = sc_v[0:1, 0:1]
    alpha1 = sc_v[1:2, 0:1]
    a1b = sc_v[2:3, 0:1]
    X = z0_v.shape[1]
    copies = []
    for c in range(3):
        for x in range(X):
            xb[c, x] = along * z0_v[c, x] + alpha1 * z1_v[c, x]
            rb[c, x] = r_v[c, x] - alpha1 * az_v[c, x] - a1b * y_v[c, x]
        for n, (src, dst) in enumerate(((xb, x_out), (rb, res_out))):
            copies.append(pltpu.make_async_copy(src.at[c], dst.at[c], sem.at[n, c]))
            copies[-1].start()
    for copy in copies:
        copy.wait()


def local(nw, nn, right_side, occupancy, region, coarse_inverse):
    _, X, Y, Z = right_side.shape
    ncr, NC = coarse_inverse.shape
    ND = nw * nn
    f32, i32 = jnp.float32, jnp.int32
    V = pltpu.VMEM
    field, pad, scal = (3, X, Y, Z), (3, X + 2, Y, Z), (X, Y, Z)
    scratch = [
        V(scal, i32), V(scal, i32), V((ncr, NC), f32),
        V((X + 2, Y, Z), f32), V((X + 1, Y, Z), f32),
        V(scal, f32), V(scal, f32), V(scal, f32), V(scal, f32), V(scal, f32), V(scal, f32),
        V(pad, f32), V(pad, f32),
        V((2, 3, X, Z), f32), V((2, 3, X, Z), f32),
        V((2, 2, Y, Z), i32), V((2, 2, X, Z), i32), V((2, 2, X, Z), i32),
        V((4, ncr, NC), f32),
        V((2, 2, 3, Y, Z), f32), V((2, 2, 3, Y, Z), f32),
        V((2, 2, 3, X, Z), f32), V((2, 2, 3, X, Z), f32),
        V((3, SUB, LANES), f32), V((3, ND, LANES), f32),
        pltpu.SemaphoreType.DMA((4,)),
        pltpu.SemaphoreType.DMA((5, 4)), pltpu.SemaphoreType.DMA((5, 4)),
        pltpu.SemaphoreType.DMA((3,)), pltpu.SemaphoreType.DMA((3,)),
    ]
    parts = pl.pallas_call(
        functools.partial(kernel, nw, nn),
        out_shape=(V(field, f32),) * 5 + (V((SUB, LANES), f32),),
        in_specs=[pl.BlockSpec(memory_space=pltpu.HBM)] * 4,
        out_specs=(pl.BlockSpec(memory_space=pltpu.VMEM),) * 6,
        scratch_shapes=scratch,
        compiler_params=pltpu.CompilerParams(collective_id=0, has_side_effects=True, vmem_limit_bytes=32 * 1024 * 1024),
    )(*[pltpu.with_memory_space_constraint(a, pltpu.HBM) for a in (right_side, occupancy, region, coarse_inverse)])
    return pl.pallas_call(
        finish,
        out_shape=(jax.ShapeDtypeStruct(field, f32),) * 2,
        in_specs=[pl.BlockSpec(memory_space=pltpu.VMEM)] * 6,
        out_specs=(pl.BlockSpec(memory_space=pltpu.HBM),) * 2,
        scratch_shapes=[V(field, f32), V(field, f32), pltpu.SemaphoreType.DMA((2, 3))],
        compiler_params=pltpu.CompilerParams(vmem_limit_bytes=16 * 1024 * 1024),
    )(*parts)


def solution(mesh):
    return jax.shard_map(
        functools.partial(local, mesh.shape["wide"], mesh.shape["narrow"]),
        mesh=mesh,
        in_specs=(
            P(None, "wide", "narrow", None),
            P("wide", "narrow", None),
            P("wide", "narrow", None),
            P(("wide", "narrow"), None),
        ),
        out_specs=(P(None, "wide", "narrow", None), P(None, "wide", "narrow", None)),
        check_vma=False,
    )
```

profile of v0, /device:TPU:0, one launch (start us, length us, event | category | flops | bytes accessed | tf_op | source)
XLA Modules:
  0.0 25.2 jit_solution(105507030442994510)
XLA Ops:
  0.6 23.5 %shard_map.59 = (f32[3,16,16,128]{3,2,1,0:T(8,128)S(1)}, f32[3,16,16,128]{3,2,1,0:T(8,128)S(1)}, f32[3,16,16,128]{3,2,1,0:T(8,128)S(1)}, f32[3,16,16,128]{3,2,1,...) custom-call(f32[3,16,16,128]{3,2,1,0:T(8,128)} %r_hbm.1, s32[16,16,128]{2,1,0:T(8,128)} %occ_hbm.1, ...), custom_call_target="tpu_custom_call" | custom-call | tf_op jit(solution)/shard_map/pallas_call | solution.py:428
  24.2 1.0 %shard_map.60 = (f32[3,16,16,128]{3,2,1,0:T(8,128)}, f32[3,16,16,128]{3,2,1,0:T(8,128)}) custom-call(f32[3,16,16,128]{3,2,1,0:T(8,128)S(1)} %get-tuple-element.8.z0_v, f32[3,16,16,128]{3,2,1,0:T(8,128)S(1)} %get-tuple-element.9.z1_v, f32[3,16,16,128]{3,2,1,0:T(8,128)S(1)} %get-tuple-element.10.r_v, f32[3,16,16,128]{3,2,1,0:T(8,128)S(1)} %get-tuple-element.11.az_v, ...), custom_call_target="tpu_custom_call" | custom-call | tf_op jit(solution)/shard_map/pallas_call | solution.py:436
where the time goes:
time: 25.3 us; the launch traced here: 25.2 us
  Pallas kernels  24.5 us (97%)
  between operations  0.64 us (3%)
    pallas_call x1, Pallas kernels, local(): pl.pallas_call(functools.partial(kernel, nw, nn), out_shape=(V(field, f32...  23.5 us
    pallas_call x1, Pallas kernels, local(): pl.pallas_call(finish, out_shape=(jax.ShapeDtypeStruct(field, f32),) * 2,...  0.99 us

commit v1 on v0

--- a/solution.py
+++ b/solution.py
@@ -16,12 +16,16 @@
 soft_stiff = 0.1
 
 
+def group_of(n):
+    return max(d for d in range(1, n + 1) if n % d == 0 and d * d <= n)
+
+
 def kernel(nw, nn, r_hbm, occ_hbm, reg_hbm, ci_hbm,
            z0_v, z1_v, r_v, az_v, y_v, sc_v,
             occ_v, reg_v, c_v, k_p, kx, kym, kyp, kzm, kzp, dg, invd,
            z_p, v_p, zy, vy,
            ix_in, iy_send, iy_in, c_in, wx_send, wx_in, wy_send, wy_in,
-           row_send, rows, load_sem, hs_send, hs_recv, ag_send, ag_recv):
+           row_send, rows, load_sem, hs_send, hs_recv, ag_send, ag_recv, ready):
     X, Y, Z = occ_v.shape
     ncr, NC = c_v.shape
     G = ncr // 3
@@ -31,8 +35,12 @@
     me = wi * nn + ni
     f32 = jnp.float32
 
+    GP = group_of(nw) * nn
+    NG = ND // GP
+    grp, pos = me // GP, lax.rem(me, GP)
+
     loads = [pltpu.make_async_copy(s, d, load_sem.at[i]) for i, (s, d) in enumerate(
-        ((occ_hbm, occ_v), (reg_hbm, reg_v), (r_hbm, r_v), (ci_hbm, c_v)))]
+        ((reg_hbm, reg_v), (r_hbm, r_v), (occ_hbm, occ_v), (ci_hbm, c_v)))]
     for l in loads:
         l.start()
 
@@ -42,11 +50,32 @@
 
     barrier = pltpu.get_barrier_semaphore()
 
-    def greet(i, _):
-        pl.semaphore_signal(barrier, inc=1, device_id=peer(i), device_id_type=MESH)
-        return 0
-
-    lax.fori_loop(1, ND, greet, 0, unroll=ND <= 64)
+    def at(t):
+        return (t // nn, lax.rem(t, nn))
+
+    def greet(t, _):
+        pl.semaphore_signal(barrier, inc=1, device_id=at(t), device_id_type=MESH)
+        return 0
+
+    lax.fori_loop(me + 1, ND, greet, 0)
+
+    def kind_of(low, high):
+        apart = high // GP - low // GP
+        k = jnp.where(lax.rem(high, GP) == lax.rem(low, GP), apart, NG + 1)
+        k = jnp.where(high - low == nn, NG, k)
+        return jnp.where(apart == 0, 0, k)
+
+    def wait_for(sem, count):
+        @pl.when(count > 0)
+        def _():
+            pl.semaphore_wait(sem, count)
+
+    def tell(i, _):
+        t = me - 1 - i
+        pl.semaphore_signal(ready.at[kind_of(t, me)], inc=1, device_id=at(t), device_id_type=MESH)
+        return 0
+
+    has_beside = jnp.logical_and(wi < nw - 1, kind_of(me, me + nn) == NG)
 
     has = (wi > 0, wi < nw - 1, ni > 0, ni < nn - 1)
     to = ((wi - 1, ni), (wi + 1, ni), (wi, ni - 1), (wi, ni + 1))
@@ -65,17 +94,12 @@
             else:
                 iy_in[d - 2] = jnp.zeros((2, X, Z), jnp.int32)
 
-    loads[0].wait()
-    loads[1].wait()
-
     def pack_ints(x, _):
         iy_send[0, 0, pl.ds(x, 1), :] = occ_v[x, 0:1, :]
         iy_send[1, 0, pl.ds(x, 1), :] = occ_v[x, Y - 1:Y, :]
         iy_send[0, 1, pl.ds(x, 1), :] = reg_v[x, 0:1, :]
         iy_send[1, 1, pl.ds(x, 1), :] = reg_v[x, Y - 1:Y, :]
         return 0
-
-    looped(0, X, pack_ints, 0)
 
     def fold(a):
         return jnp.sum(a.reshape(Y // SUB, SUB, Z), axis=0)
@@ -103,6 +127,36 @@
         row = jnp.sum(jnp.where(lane == target, col, 0.0), axis=0, keepdims=True)
         row_send[p, 0:1, :] = row
         rows[p, pl.ds(me, 1), :] = row
+
+    def group_start():
+        def send(i, _):
+            pltpu.make_async_remote_copy(
+                src_ref=row_send.at[0, pl.ds(0, 1)], dst_ref=rows.at[0, pl.ds(me, 1)],
+                send_sem=ag_send.at[0], recv_sem=ag_recv.at[0],
+                device_id=at(grp * GP + lax.rem(pos + i, GP)), device_id_type=MESH).start()
+            return 0
+        lax.fori_loop(1, GP, send, 0, unroll=GP <= 64)
+
+    def group_wait(sem):
+        part = rows.at[0, pl.ds(0, GP - 1)]
+        pltpu.make_async_copy(part, part, sem.at[0]).wait()
+
+    def across_start():
+        mine = rows.at[0, pl.ds(pl.multiple_of(grp * GP, GP), GP)]
+        for k in range(1, NG):
+            for up in (True, False):
+                @pl.when(grp + k < NG if up else grp >= k)
+                def _():
+                    if up and k * GP != nn:
+                        pl.semaphore_wait(ready.at[k], 1)
+                    pltpu.make_async_remote_copy(
+                        src_ref=mine, dst_ref=mine,
+                        send_sem=ag_send.at[3], recv_sem=ag_recv.at[3],
+                        device_id=at(me + (k * GP if up else -k * GP)), device_id_type=MESH).start()
+
+    def across_wait(sem):
+        part = rows.at[0, pl.ds(0, ND - GP)]
+        pltpu.make_async_copy(part, part, sem.at[3]).wait()
 
     def gather_start(p):
         def send(i, _):
@@ -194,16 +248,28 @@
                 for c in copies(kind, d):
                     c.wait_send()
 
-    loads[2].wait()
+    loads[0].wait()
+    loads[1].wait()
     acc = looped(0, X, lambda x, a: add_rc(a, reg_v[x], [r_v[c, x] for c in range(3)]),
                         zero_acc(ncr))
     make_row(0, acc, 0)
+
+    wait_for(barrier, me)
+    lax.fori_loop(0, me, tell, 0)
+    wait_for(ready.at[0], GP - 1 - pos)
+    group_start()
+    loads[2].wait()
+    looped(0, X, pack_ints, 0)
+
+    @pl.when(has_beside)
+    def _():
+        pl.semaphore_wait(ready.at[NG], 1)
+
+    halo_start(0)
     loads[3].wait()
-
-    pl.semaphore_wait(barrier, ND - 1)
-    halo_start(0)
-    gather_start(0)
     halo_start(1)
+    group_wait(ag_recv)
+    across_start()
 
     def stiff_of(o):
         return soft_stiff + (bone_stiff - soft_stiff) * o.astype(f32)
@@ -297,7 +363,7 @@
             out.append(a)
         return u, out
 
-    gather_wait(0, ag_recv)
+    across_wait(ag_recv)
     halo_wait(1)
     tiles = coarse_vector(0)
     q = answers(tiles, c_v)
@@ -332,6 +398,10 @@
 
     acc = looped(0, X, first, zero_acc(ncr + 2))
     make_row(1, acc, 0)
+    rest = ND - 1 - me - (GP - 1 - pos) - (NG - 1 - grp)
+    if GP != nn:
+        rest = rest - jnp.where(has_beside, 1, 0)
+    wait_for(ready.at[NG + 1], rest)
     gather_start(1)
     for c in range(3):
         wx_send[1, 0, c] = v_p[c, 1]
@@ -382,7 +452,9 @@
     sc_v[2:3, :] = jnp.broadcast_to(a1b, (1, LANES))
     for kind in range(4):
         halo_done(kind)
-    for p in range(3):
+    group_wait(ag_send)
+    across_wait(ag_send)
+    for p in range(1, 3):
         gather_wait(p, ag_send)
 
 
@@ -423,7 +495,8 @@
         V((3, SUB, LANES), f32), V((3, ND, LANES), f32),
         pltpu.SemaphoreType.DMA((4,)),
         pltpu.SemaphoreType.DMA((5, 4)), pltpu.SemaphoreType.DMA((5, 4)),
-        pltpu.SemaphoreType.DMA((3,)), pltpu.SemaphoreType.DMA((3,)),
+        pltpu.SemaphoreType.DMA((4,)), pltpu.SemaphoreType.DMA((4,)),
+        pltpu.SemaphoreType.REGULAR((nw // group_of(nw) + 2,)),
     ]
     parts = pl.pallas_call(
         functools.partial(kernel, nw, nn),

time: 25.3 us -> 25.8 us (1.020)
  Pallas kernels: 24.5 us -> 25 us
    pallas_call x1, Pallas kernels: 23.5 us -> 24 us  [local(): pl.pallas_call(functools.partial(kernel, nw, nn), out_shape=(V(field, f32...]
where the time goes in v1:
time: 25.8 us; the launch traced here: 25.7 us
  Pallas kernels  25 us (97%)
  between operations  0.64 us (2%)
    pallas_call x1, Pallas kernels, local(): pl.pallas_call(functools.partial(kernel, nw, nn), out_shape=(V(field, f32...  24 us
    pallas_call x1, Pallas kernels, local(): pl.pallas_call(finish, out_shape=(jax.ShapeDtypeStruct(field, f32),) * 2,...  0.99 us

profile of v1, /device:TPU:0, one launch (start us, length us, event | category | flops | bytes accessed | tf_op | source)
XLA Modules:
  0.0 25.7 jit_solution(17355784149551936031)
XLA Ops:
  0.6 24.0 %shard_map.59 = (f32[3,16,16,128]{3,2,1,0:T(8,128)S(1)}, f32[3,16,16,128]{3,2,1,0:T(8,128)S(1)}, f32[3,16,16,128]{3,2,1,0:T(8,128)S(1)}, f32[3,16,16,128]{3,2,1,...) custom-call(f32[3,16,16,128]{3,2,1,0:T(8,128)} %r_hbm.1, s32[16,16,128]{2,1,0:T(8,128)} %occ_hbm.1, ...), custom_call_target="tpu_custom_call" | custom-call | tf_op jit(solution)/shard_map/pallas_call | solution.py:501
  24.7 1.0 %shard_map.60 = (f32[3,16,16,128]{3,2,1,0:T(8,128)}, f32[3,16,16,128]{3,2,1,0:T(8,128)}) custom-call(f32[3,16,16,128]{3,2,1,0:T(8,128)S(1)} %get-tuple-element.8.z0_v, f32[3,16,16,128]{3,2,1,0:T(8,128)S(1)} %get-tuple-element.9.z1_v, f32[3,16,16,128]{3,2,1,0:T(8,128)S(1)} %get-tuple-element.10.r_v, f32[3,16,16,128]{3,2,1,0:T(8,128)S(1)} %get-tuple-element.11.az_v, ...), custom_call_target="tpu_custom_call" | custom-call | tf_op jit(solution)/shard_map/pallas_call | solution.py:509

commit v2 on v0

--- a/solution.py
+++ b/solution.py
@@ -16,7 +16,7 @@
 soft_stiff = 0.1
 
 
-def kernel(nw, nn, r_hbm, occ_hbm, reg_hbm, ci_hbm,
+def kernel_wide(nw, nn, r_hbm, occ_hbm, reg_hbm, ci_hbm,
            z0_v, z1_v, r_v, az_v, y_v, sc_v,
             occ_v, reg_v, c_v, k_p, kx, kym, kyp, kzm, kzp, dg, invd,
            z_p, v_p, zy, vy,
@@ -386,7 +386,7 @@
         gather_wait(p, ag_send)
 
 
-def finish(z0_v, z1_v, r_v, az_v, y_v, sc_v, x_out, res_out, xb, rb, sem):
+def finish_wide(z0_v, z1_v, r_v, az_v, y_v, sc_v, x_out, res_out, xb, rb, sem):
     along = sc_v[0:1, 0:1]
     alpha1 = sc_v[1:2, 0:1]
     a1b = sc_v[2:3, 0:1]
@@ -403,7 +403,7 @@
         copy.wait()
 
 
-def local(nw, nn, right_side, occupancy, region, coarse_inverse):
+def local_wide(nw, nn, right_side, occupancy, region, coarse_inverse):
     _, X, Y, Z = right_side.shape
     ncr, NC = coarse_inverse.shape
     ND = nw * nn
@@ -426,7 +426,7 @@
         pltpu.SemaphoreType.DMA((3,)), pltpu.SemaphoreType.DMA((3,)),
     ]
     parts = pl.pallas_call(
-        functools.partial(kernel, nw, nn),
+        functools.partial(kernel_wide, nw, nn),
         out_shape=(V(field, f32),) * 5 + (V((SUB, LANES), f32),),
         in_specs=[pl.BlockSpec(memory_space=pltpu.HBM)] * 4,
         out_specs=(pl.BlockSpec(memory_space=pltpu.VMEM),) * 6,
@@ -434,13 +434,663 @@
         compiler_params=pltpu.CompilerParams(collective_id=0, has_side_effects=True, vmem_limit_bytes=32 * 1024 * 1024),
     )(*[pltpu.with_memory_space_constraint(a, pltpu.HBM) for a in (right_side, occupancy, region, coarse_inverse)])
     return pl.pallas_call(
-        finish,
+        finish_wide,
         out_shape=(jax.ShapeDtypeStruct(field, f32),) * 2,
         in_specs=[pl.BlockSpec(memory_space=pltpu.VMEM)] * 6,
         out_specs=(pl.BlockSpec(memory_space=pltpu.HBM),) * 2,
         scratch_shapes=[V(field, f32), V(field, f32), pltpu.SemaphoreType.DMA((2, 3))],
         compiler_params=pltpu.CompilerParams(vmem_limit_bytes=16 * 1024 * 1024),
     )(*parts)
+
+
+REPLICATED_BYTES = 4 * 1024 * 1024
+DEEP = 3
+AROUND = ((-1, 0), (1, 0), (0, -1), (0, 1), (-1, -1), (-1, 1), (1, -1), (1, 1))
+BACK = tuple(AROUND.index((-a, -b)) for a, b in AROUND)
+
+
+def group_of(n):
+    return max(d for d in range(1, n + 1) if n % d == 0 and d * d <= n)
+
+
+def spread_over(reg, q, G):
+    masks = [reg == g for g in range(G)]
+    out = []
+    for c in range(3):
+        s = jnp.zeros(reg.shape, jnp.float32)
+        for g in range(G):
+            s = jnp.where(masks[g], q[g * 3 + c], s)
+        out.append(s)
+    return out
+
+
+def stencil(u, prev, after, faces, x, rows):
+    kx, kym, kyp, kzm, kzp = faces
+    YE, Z = u.shape
+    low, high = pltpu.roll(u, 1, 0)[0:rows], pltpu.roll(u, YE - 1, 0)[0:rows]
+    v = u[0:rows]
+    a = kx[x, 0:rows] * prev[0:rows] + kx[x + 1, 0:rows] * after[0:rows]
+    a = a + (kym[x, 0:rows] * low + kyp[x, 0:rows] * high)
+    return a + (kzm[x, 0:rows] * pltpu.roll(v, 1, 1) + kzp[x, 0:rows] * pltpu.roll(v, Z - 1, 1))
+
+
+def kernel(nw, nn, r_hbm, occ_hbm, reg_hbm, ci_hbm,
+           z_o, g_o, r_o, y_o, ag_o, reg_o, k4, dg, kx, kym, kyp, kzm, kzp, q_o, sc_o,
+           occ_e, reg_e, r_e, k_e, invd, z_e, g_e,
+           call, c_in, qpair, row_send, rows, ac_send, ac,
+           load_sem, hs_send, hs_recv, hc_send, hc_recv, ag_send, ag_recv, cs_send, cs_recv, ready):
+    E, YE, Z = occ_e.shape
+    X, Y = E - 2 * DEEP, YE - SUB
+    ncr, NC = c_in.shape[1:]
+    G = ncr // 3
+    ND = nw * nn
+    NH = ND // 2
+    wi = lax.axis_index("wide")
+    ni = lax.axis_index("narrow")
+    me = wi * nn + ni
+    half, slot = lax.rem(wi, 2), (wi // 2) * nn + ni
+    f32 = jnp.float32
+    GP = group_of(nw) * nn
+    NG = ND // GP
+    grp, pos = me // GP, lax.rem(me, GP)
+    own = pl.ds(DEEP, X)
+
+    loads = [pltpu.make_async_copy(s, d, load_sem.at[i]) for i, (s, d) in enumerate((
+        (reg_hbm, reg_e.at[own, pl.ds(0, Y)]), (r_hbm, r_e.at[:, own, pl.ds(0, Y)]),
+        (occ_hbm, occ_e.at[own, pl.ds(0, Y)]), (ci_hbm, call.at[half, slot])))]
+    for l in loads:
+        l.start()
+
+    barrier = pltpu.get_barrier_semaphore()
+
+    def at(t):
+        return (t // nn, lax.rem(t, nn))
+
+    def wait_for(sem, count):
+        @pl.when(count > 0)
+        def _():
+            pl.semaphore_wait(sem, count)
+
+    def greet(t, _):
+        pl.semaphore_signal(barrier, inc=1, device_id=at(t), device_id_type=MESH)
+        return 0
+
+    lax.fori_loop(me + 1, ND, greet, 0)
+
+    def kind_of(low, high):
+        apart = high // GP - low // GP
+        k = jnp.where(lax.rem(high, GP) == lax.rem(low, GP), apart, NG + 1)
+        aside = lax.rem(high, nn) - lax.rem(low, nn)
+        touch = jnp.logical_and(high // nn - low // nn == 1, jnp.logical_and(aside >= -1, aside <= 1))
+        k = jnp.where(touch, NG, k)
+        return jnp.where(apart == 0, 0, k)
+
+    def tell(i, _):
+        t = me - 1 - i
+        pl.semaphore_signal(ready.at[kind_of(t, me)], inc=1, device_id=at(t), device_id_type=MESH)
+        return 0
+
+    has = []
+    for a, b in AROUND:
+        h = jnp.logical_and(wi + a >= 0, wi + a < nw)
+        has.append(jnp.logical_and(h, jnp.logical_and(ni + b >= 0, ni + b < nn)))
+
+    def part(arr, d, into):
+        a, b = AROUND[d]
+        deep = {0: DEEP, 1: 2, 2: 2}[arr] if a == 0 or b == 0 else {0: 2, 1: 1, 2: 1}[arr]
+        if into:
+            xs = {-1: (DEEP - deep, deep), 0: (DEEP, X), 1: (DEEP + X, deep)}[a]
+            ys = {-1: (YE - deep, deep), 0: (0, Y), 1: (Y, deep)}[b]
+        else:
+            xs = {-1: (DEEP, deep), 0: (DEEP, X), 1: (DEEP + X - deep, deep)}[a]
+            ys = {-1: (0, deep), 0: (0, Y), 1: (Y - deep, deep)}[b]
+        xs, ys = pl.ds(*xs), pl.ds(*ys)
+        return (slice(None), xs, ys) if arr == 2 else (xs, ys)
+
+    fields = (occ_e, reg_e, r_e)
+    for d in range(8):
+        @pl.when(jnp.logical_not(has[d]))
+        def _():
+            for n, ref in enumerate(fields):
+                where = part(n, d, True)
+                v = ref[where]
+                ref[where] = jnp.full(v.shape, (-1, -1, 0)[n], v.dtype)
+            c_in[d] = jnp.zeros((ncr, NC), f32)
+
+    wait_for(barrier, me)
+    lax.fori_loop(0, me, tell, 0)
+
+    def fold(a):
+        return jnp.sum(a.reshape(a.shape[0] // SUB, SUB, Z), axis=0)
+
+    def zero_acc(n):
+        return tuple(jnp.zeros((SUB, Z), f32) for _ in range(n))
+
+    def add_rc(acc, reg, u):
+        out = list(acc)
+        for g in range(G):
+            m = reg == g
+            for c in range(3):
+                out[g * 3 + c] = acc[g * 3 + c] + fold(jnp.where(m, u[c], 0.0))
+        return out
+
+    base = (me * ncr) % LANES
+
+    def column(acc):
+        a = jnp.concatenate([jnp.sum(b, axis=0, keepdims=True) for b in acc], axis=0)
+        return jnp.sum(a, axis=1, keepdims=True)
+
+    def make_row(p, acc):
+        col = column(acc)
+        n = len(acc)
+        k = lax.broadcasted_iota(jnp.int32, (n, LANES), 0)
+        lane = lax.broadcasted_iota(jnp.int32, (n, LANES), 1)
+        target = (base + k) & (LANES - 1)
+        row = jnp.sum(jnp.where(lane == target, col, 0.0), axis=0, keepdims=True)
+        row_send[p, 0:1, :] = row
+        rows[p, pl.ds(me, 1), :] = row
+
+    def row_to(p, t, sem):
+        pltpu.make_async_remote_copy(
+            src_ref=row_send.at[p, pl.ds(0, 1)], dst_ref=rows.at[p, pl.ds(me, 1)],
+            send_sem=ag_send.at[sem], recv_sem=ag_recv.at[sem],
+            device_id=at(t), device_id_type=MESH).start()
+
+    def rows_wait(p, count, sem):
+        if count:
+            some = rows.at[p, pl.ds(0, count)]
+            pltpu.make_async_copy(some, some, sem).wait()
+
+    def by_group(count, sem):
+        for n in range(NG):
+            @pl.when(grp == n)
+            def _():
+                rows_wait(0, count(n), sem)
+
+    def each_peer(send):
+        def body(i, _):
+            send(lax.rem(me + i, ND))
+            return 0
+        lax.fori_loop(1, ND, body, 0, unroll=ND <= 64)
+
+    loads[0].wait()
+    loads[1].wait()
+    acc = looped(0, X, lambda x, a: tuple(add_rc(
+        a, reg_e[x + DEEP, 0:Y], [r_e[c, x + DEEP, 0:Y] for c in range(3)])), zero_acc(ncr))
+    make_row(0, acc)
+
+    wait_for(ready.at[0], GP - 1 - pos)
+
+    def inside(i, _):
+        row_to(0, grp * GP + lax.rem(pos + i, GP), 0)
+        return 0
+
+    def below(i, _):
+        row_to(0, grp * GP - 1 - i, 2)
+        return 0
+
+    lax.fori_loop(1, GP, inside, 0, unroll=GP <= 64)
+    lax.fori_loop(0, grp * GP, below, 0)
+
+    def halo(n, d):
+        a, b = AROUND[d]
+        e = BACK[d]
+        return pltpu.make_async_remote_copy(
+            src_ref=fields[n].at[part(n, d, False)], dst_ref=fields[n].at[part(n, e, True)],
+            send_sem=hs_send.at[n, d], recv_sem=hs_recv.at[n, e],
+            device_id=(wi + a, ni + b), device_id_type=MESH)
+
+    def halo_c(d):
+        a, b = AROUND[d]
+        return pltpu.make_async_remote_copy(
+            src_ref=call.at[half, slot], dst_ref=c_in.at[BACK[d]],
+            send_sem=hc_send.at[d], recv_sem=hc_recv.at[BACK[d]],
+            device_id=(wi + a, ni + b), device_id_type=MESH)
+
+    def arrived(n, d):
+        where = part(n, d, True)
+        pltpu.make_async_remote_copy(
+            src_ref=fields[n].at[where], dst_ref=fields[n].at[where],
+            send_sem=hs_send.at[n, d], recv_sem=hs_recv.at[n, d],
+            device_id=(wi, ni), device_id_type=MESH).wait_recv()
+
+    beside = jnp.where(kind_of(me, me + nn) == NG, 1, 0)
+    touching = jnp.where(wi < nw - 1, beside * (
+        1 + jnp.where(ni > 0, 1, 0) + jnp.where(ni < nn - 1, 1, 0)), 0)
+    loads[2].wait()
+    wait_for(ready.at[NG], touching)
+    for n in range(3):
+        for d in range(8):
+            @pl.when(has[d])
+            def _():
+                halo(n, d).start()
+    loads[3].wait()
+    for d in range(8):
+        @pl.when(has[d])
+        def _():
+            halo_c(d).start()
+
+    rows_wait(0, GP - 1, ag_recv.at[0])
+    mine = rows.at[0, pl.ds(pl.multiple_of(grp * GP, GP), GP)]
+    for k in range(1, NG):
+        @pl.when(grp + k < NG)
+        def _():
+            if k * GP != nn:
+                pl.semaphore_wait(ready.at[k], 1)
+            pltpu.make_async_remote_copy(
+                src_ref=mine, dst_ref=mine, send_sem=ag_send.at[1], recv_sem=ag_recv.at[1],
+                device_id=at(me + k * GP), device_id_type=MESH).start()
+
+    rest = ND - 1 - me - (GP - 1 - pos) - touching
+    if GP != nn:
+        rest = rest - (NG - 1 - grp)
+    wait_for(ready.at[NG + 1], rest)
+
+    def send_c(i, _):
+        t = lax.rem(slot + i, NH)
+        pltpu.make_async_remote_copy(
+            src_ref=call.at[half, slot], dst_ref=call.at[half, slot],
+            send_sem=cs_send.at[0], recv_sem=cs_recv.at[0],
+            device_id=((t // nn) * 2 + half, lax.rem(t, nn)), device_id_type=MESH).start()
+        return 0
+
+    lax.fori_loop(1, NH, send_c, 0)
+
+    for n in range(3):
+        for d in range(8):
+            @pl.when(has[d])
+            def _():
+                arrived(n, d)
+
+    lane_id = lax.broadcasted_iota(jnp.int32, (YE, Z), 1)
+
+    def stiffness(x, _):
+        o = occ_e[x]
+        k_e[x] = jnp.where(o < 0, 0.0, soft_stiff + (bone_stiff - soft_stiff) * o.astype(f32))
+        return 0
+
+    lax.fori_loop(0, E, stiffness, 0, unroll=True)
+
+    def pairs(acc, first, second, value):
+        out = list(acc)
+        for g in range(G):
+            t = jnp.where(second == g, value, 0.0)
+            for h in range(G):
+                out[h * G + g] = acc[h * G + g] + fold(jnp.where(first == h, t, 0.0))
+        return out
+
+    row8 = lax.broadcasted_iota(jnp.int32, (SUB, Z), 0)
+
+    def coefficients(x):
+        k = k_e[x]
+        low, high = pltpu.roll(k, 1, 0), pltpu.roll(k, YE - 1, 0)
+        back = jnp.where(lane_id == 0, 0.0, pltpu.roll(k, 1, 1))
+        ahead = jnp.where(lane_id == Z - 1, 0.0, pltpu.roll(k, Z - 1, 1))
+        xm = 0.5 * (k + k_e[x - 1])
+        xp = 0.5 * (k + k_e[x + 1])
+        ym = 0.5 * (k + low)
+        yp = 0.5 * (k + high)
+        zm = 0.5 * (k + back)
+        zp = 0.5 * (k + ahead)
+        diag = xm + xp + ym + yp + zm + zp + 0.5 * k
+        inv = jnp.where(k > 0.0, 1.0 / diag, 0.0)
+        zp = jnp.where(lane_id == Z - 1, 0.0, zp)
+        kx[x] = xm
+        kx[x + 1] = xp
+        kym[x] = ym
+        kyp[x] = yp
+        kzm[x] = jnp.where(lane_id == 0, 0.0, zm)
+        kzp[x] = zp
+        d = diag - 0.25 * k
+        dg[x] = d
+        k4[x] = 0.25 * k
+        invd[x] = inv
+        reg_o[x] = reg_e[x]
+        for c in range(3):
+            z_e[c, x] = r_e[c, x] * inv
+        return xp, yp, zp, d, 0.25 * k
+
+    def edge_plane(x):
+        coefficients(x)
+
+    for x in (1, 2, DEEP + X, DEEP + X + 1):
+        edge_plane(x)
+
+    n2 = G * G
+
+    def inner(i, carry):
+        x = i + DEEP
+        xp, yp, zp, d, kq = coefficients(x)
+        reg = reg_e[x]
+        r16 = reg[0:Y]
+        up = pltpu.roll(reg, YE - 1, 0)
+        inside_x = jnp.where(i < X - 1, xp[0:Y], 0.0)
+        to_x = xp[0:Y] - inside_x
+        last = yp[Y - SUB:Y]
+        inside_y = jnp.concatenate([yp[0:Y - SUB], jnp.where(row8 == SUB - 1, 0.0, last)], axis=0)
+        to_y = jnp.where(row8 == SUB - 1, last, 0.0)
+        ahead = pltpu.roll(r16, Z - 1, 1)
+        after = reg_e[x + 1, 0:Y]
+        own_acc, x_acc, y_acc = list(carry[:n2]), list(carry[n2:2 * n2]), list(carry[2 * n2:3 * n2])
+        sums = list(carry[3 * n2:])
+        for g in range(G):
+            t = jnp.where(after == g, inside_x, 0.0) + jnp.where(up[0:Y] == g, inside_y, 0.0)
+            t = t + jnp.where(ahead == g, zp[0:Y], 0.0)
+            for h in range(G):
+                own_acc[h * G + g] = own_acc[h * G + g] + fold(jnp.where(r16 == h, t, 0.0))
+            m = r16 == g
+            sums[g] = sums[g] + fold(jnp.where(m, d[0:Y], 0.0))
+            sums[G + g] = sums[G + g] + fold(jnp.where(m, kq[0:Y], 0.0))
+        y_acc = pairs(y_acc, r16[Y - SUB:Y], up[Y - SUB:Y], to_y)
+        return tuple(own_acc) + tuple(x_acc) + tuple(y_acc) + tuple(sums)
+
+    acc = lax.fori_loop(0, X, inner, zero_acc(3 * n2 + 2 * G), unroll=2)
+    top = DEEP + X - 1
+    x_acc = pairs(zero_acc(n2), reg_e[top, 0:Y], reg_e[top + 1, 0:Y], kx[top + 1, 0:Y])
+    cols = [column(acc[:n2]), column(x_acc), column(acc[2 * n2:3 * n2]), column(acc[3 * n2:])]
+
+    lane = lax.broadcasted_iota(jnp.int32, (n2, LANES), 1)
+    pair = lax.broadcasted_iota(jnp.int32, (n2, LANES), 0)
+    at_pair = jnp.logical_and(lane >= 3 * pair, lane < 3 * pair + 3)
+
+    def lanes_of(col, mask):
+        return jnp.sum(jnp.where(mask, col, 0.0), axis=0, keepdims=True)
+
+    lane_g = lax.broadcasted_iota(jnp.int32, (2 * G, LANES), 1)
+    row_g = lax.broadcasted_iota(jnp.int32, (2 * G, LANES), 0)
+    start = jnp.where(row_g < G, 3 * (G + 1) * row_g, 3 * n2 + 9 * (row_g - G))
+    at_sum = jnp.logical_and(lane_g >= start, lane_g < start + jnp.where(row_g < G, 3, 9))
+    ac_rows = (lanes_of(cols[0], at_pair) * -2.0 + lanes_of(cols[3], at_sum),
+               lanes_of(cols[1], at_pair) * -2.0, lanes_of(cols[2], at_pair) * -2.0)
+    for n in range(3):
+        ac_send[n, 0:1, :] = ac_rows[n]
+        ac[n, pl.ds(me, 1), :] = ac_rows[n]
+
+    def send_ac(t):
+        pltpu.make_async_remote_copy(
+            src_ref=ac_send.at[:, pl.ds(0, 1)], dst_ref=ac.at[:, pl.ds(me, 1)],
+            send_sem=ag_send.at[4], recv_sem=ag_recv.at[4],
+            device_id=at(t), device_id_type=MESH).start()
+
+    each_peer(send_ac)
+
+    def coarse_vector(block):
+        tiles = []
+        for t in range(NC // LANES):
+            lo = (LANES * t) // ncr // SUB * SUB
+            hi = min(ND, -(-(-(-(LANES * (t + 1)) // ncr)) // SUB) * SUB)
+            d = lax.broadcasted_iota(jnp.int32, (hi - lo, LANES), 0) + lo
+            j = lax.broadcasted_iota(jnp.int32, (hi - lo, LANES), 1) + LANES * t
+            m = (j >= d * ncr) & (j < d * ncr + ncr)
+            tiles.append(jnp.sum(jnp.where(m, block[lo:hi, :], 0.0), axis=0, keepdims=True))
+        return tiles
+
+    def total(block, s):
+        d = lax.broadcasted_iota(jnp.int32, (ND, LANES), 0)
+        lane = lax.broadcasted_iota(jnp.int32, (ND, LANES), 1)
+        m = lane == ((d * ncr + ncr + s) & (LANES - 1))
+        v = jnp.sum(jnp.where(m, block, 0.0), axis=0, keepdims=True)
+        return jnp.sum(v, axis=1, keepdims=True)
+
+    def solve(tiles, block):
+        s = block[:, 0:LANES] * tiles[0]
+        for t in range(1, len(tiles)):
+            s = s + block[:, t * LANES:(t + 1) * LANES] * tiles[t]
+        return jnp.sum(s, axis=1, keepdims=True)
+
+    def as_list(q):
+        return [q[i:i + 1, :] for i in range(ncr)]
+
+    by_group(lambda n: (NG - 1 - n) * GP, ag_recv.at[2])
+    by_group(lambda n: n * GP, ag_recv.at[1])
+    for d in range(8):
+        @pl.when(has[d])
+        def _():
+            pltpu.make_async_remote_copy(
+                src_ref=c_in.at[d], dst_ref=c_in.at[d], send_sem=hc_send.at[d], recv_sem=hc_recv.at[d],
+                device_id=(wi, ni), device_id_type=MESH).wait_recv()
+    tiles = coarse_vector(rows[0])
+    q = as_list(solve(tiles, call[half, slot]))
+    qn = [as_list(solve(tiles, c_in[d])) for d in range(8)]
+
+    def either(hi, lo):
+        return [jnp.where(row8 < SUB // 2, a, b) for a, b in zip(hi, lo)]
+
+    def add_spread(x, q_in, q_out):
+        s = spread_over(reg_e[x, 0:Y], q_in, G)
+        t = spread_over(reg_e[x, Y:YE], q_out, G)
+        for c in range(3):
+            z_e[c, x, 0:Y] = z_e[c, x, 0:Y] + s[c]
+            z_e[c, x, Y:YE] = z_e[c, x, Y:YE] + t[c]
+
+    q_side = either(qn[3], qn[2])
+
+    def spread_own(i, _):
+        add_spread(i + DEEP, q, q_side)
+        return 0
+
+    looped(0, X, spread_own, 0)
+    q_low, q_high = either(qn[5], qn[4]), either(qn[7], qn[6])
+    for x in (1, 2):
+        add_spread(x, qn[0], q_low)
+    for x in (DEEP + X, DEEP + X + 1):
+        add_spread(x, qn[1], q_high)
+
+    faces = (kx, kym, kyp, kzm, kzp)
+
+    def apply(ref, x, rows_):
+        u = [ref[c, x] for c in range(3)]
+        kk = k4[x, 0:rows_] * (u[0] + u[1] + u[2])[0:rows_]
+        return u, [dg[x, 0:rows_] * u[c][0:rows_] + kk
+                   - stencil(u[c], ref[c, x - 1], ref[c, x + 1], faces, x, rows_) for c in range(3)]
+
+    def dots(a, b):
+        return fold(a[0] * b[0] + a[1] * b[1] + a[2] * b[2])
+
+    for x in (DEEP - 1, DEEP + X):
+        _, a = apply(z_e, x, YE)
+        for c in range(3):
+            g_e[c, x] = a[c] * invd[x]
+
+    def first(i, carry):
+        x = i + DEEP
+        u, a = apply(z_e, x, YE)
+        w = []
+        for c in range(3):
+            w.append(a[c] * invd[x])
+            g_e[c, x] = w[c]
+        y = [a[c][0:Y] for c in range(3)]
+        u = [u[c][0:Y] for c in range(3)]
+        w = [w[c][0:Y] for c in range(3)]
+        r = [r_e[c, x, 0:Y] for c in range(3)]
+        for c in range(3):
+            y_o[c, i] = y[c]
+            z_o[c, i] = u[c]
+            g_o[c, i] = w[c]
+            r_o[c, i] = r[c]
+        acc = add_rc(carry[:ncr], reg_e[x, 0:Y], y)
+        return tuple(acc) + (carry[ncr] + dots(r, u), carry[ncr + 1] + dots(y, u), carry[ncr + 2] + dots(y, w))
+
+    acc1 = lax.fori_loop(0, X, first, zero_acc(ncr + 3), unroll=4)
+
+    def second(i, carry):
+        x = i + DEEP
+        w, a = apply(g_e, x, Y)
+        for c in range(3):
+            ag_o[c, i] = a[c]
+        acc = add_rc(carry[:ncr], reg_e[x, 0:Y], a)
+        return tuple(acc) + (carry[ncr] + dots([v[0:Y] for v in w], a),)
+
+    acc2 = lax.fori_loop(0, X, second, zero_acc(ncr + 1), unroll=4)
+    make_row(1, tuple(acc1) + (acc2[ncr],) + tuple(acc2[:ncr]))
+    each_peer(lambda t: row_to(1, t, 3))
+
+    others = call.at[half, pl.ds(0, NH - 1)]
+    pltpu.make_async_copy(others, others, cs_recv.at[0]).wait()
+    swap = pltpu.make_async_remote_copy(
+        src_ref=call.at[half], dst_ref=call.at[half], send_sem=cs_send.at[1], recv_sem=cs_recv.at[1],
+        device_id=(wi + 1 - 2 * half, ni), device_id_type=MESH)
+    swap.start()
+    some = ac.at[:, pl.ds(0, ND - 1)]
+    pltpu.make_async_copy(some, some, ag_recv.at[4]).wait()
+    swap.wait_recv()
+    rows_wait(1, ND - 1, ag_recv.at[3])
+
+    block = rows[1]
+    b1 = coarse_vector(block)
+    h1 = coarse_vector(pltpu.roll(block, LANES - ncr - 4, 1))
+    rr = lax.broadcasted_iota(jnp.int32, (ncr, LANES), 0)
+    ll = lax.broadcasted_iota(jnp.int32, (ncr, LANES), 1)
+    m0, m1 = rr < 0, rr < 0
+    for h in range(G):
+        for g in range(G):
+            for c in range(3):
+                k = (h * G + g) * 3 + c
+                m0 = jnp.logical_or(m0, (ll == k) & (rr == h * 3 + c))
+                m1 = jnp.logical_or(m1, (ll == k) & (rr == g * 3 + c))
+        for c in range(3):
+            for e in range(3):
+                k = 3 * n2 + h * 9 + c * 3 + e
+                m0 = jnp.logical_or(m0, (ll == k) & (rr == h * 3 + c))
+                m1 = jnp.logical_or(m1, (ll == k) & (rr == h * 3 + e))
+    lines = [jnp.zeros((1, LANES), f32) for _ in b1]
+    for w in range(nw):
+        for n in range(nn):
+            d = w * nn + n
+            q1 = solve(b1, call[w % 2, (w // 2) * nn + n])
+            qpair[0, d:d + 1, :] = jnp.sum(jnp.where(m0, q1, 0.0), axis=0, keepdims=True)
+            qpair[1, d:d + 1, :] = jnp.sum(jnp.where(m1, q1, 0.0), axis=0, keepdims=True)
+            for t in range(d * ncr // LANES, (d * ncr + ncr - 1) // LANES + 1):
+                lines[t] = lines[t] + jnp.sum(jnp.where(ll + LANES * t == rr + d * ncr, q1, 0.0), axis=0, keepdims=True)
+    first_q, second_q = qpair[0], qpair[1]
+    dev = lax.broadcasted_iota(jnp.int32, (ND, LANES), 0)
+    next_x = jnp.where(dev < ND - nn, pltpu.roll(second_q, ND - nn, 0), 0.0)
+    next_y = jnp.where(dev < ND - 1, pltpu.roll(second_q, ND - 1, 0), 0.0)
+    energy = jnp.sum(first_q * (ac[0] * second_q + ac[1] * next_x + ac[2] * next_y), axis=0, keepdims=True)
+    for t in range(len(b1)):
+        energy = energy + 2.0 * h1[t] * lines[t]
+    yv = b1[0] * lines[0]
+    for t in range(1, len(b1)):
+        yv = yv + b1[t] * lines[t]
+    yv = total(block, 2) + jnp.sum(yv, axis=1, keepdims=True)
+    vav = total(block, 3) + jnp.sum(energy, axis=1, keepdims=True)
+    rz0, zy = total(block, 0), total(block, 1)
+    alpha0 = rz0 / zy
+    rz1 = alpha0 * alpha0 * yv - rz0
+    zaz = zy - 2.0 * alpha0 * yv + alpha0 * alpha0 * vav
+    beta = rz1 / rz0
+    alpha1 = rz1 / (zaz - beta * rz1 / alpha0)
+    a1b = alpha1 * beta
+    for n, v in enumerate((alpha0 + a1b + alpha1, alpha1 * alpha0)):
+        sc_o[n:n + 1, :] = jnp.broadcast_to(v, (1, LANES))
+    q_o[0] = jnp.broadcast_to(solve(b1, call[half, slot]), (ncr, LANES))
+    for d in range(4):
+        q_o[d + 1] = jnp.broadcast_to(solve(b1, c_in[d]), (ncr, LANES))
+
+    rows_wait(0, GP - 1, ag_send.at[0])
+    by_group(lambda n: n * GP, ag_send.at[2])
+    by_group(lambda n: (NG - 1 - n) * GP, ag_send.at[1])
+    rows_wait(1, ND - 1, ag_send.at[3])
+    pltpu.make_async_copy(some, some, ag_send.at[4]).wait()
+    pltpu.make_async_copy(others, others, cs_send.at[0]).wait()
+    swap.wait_send()
+    for d in range(8):
+        @pl.when(has[d])
+        def _():
+            for n in range(3):
+                halo(n, d).wait_send()
+            halo_c(d).wait_send()
+
+
+def finish(z_v, g_v, r_v, y_v, ag_v, reg_v, k4, dg, kx, kym, kyp, kzm, kzp, q_v, sc_v, x_out, res_out, s_e, xb, rb, sem):
+    a, b = sc_v[0:1, 0:1], sc_v[1:2, 0:1]
+    E, YE, Z = reg_v.shape
+    X, Y = E - 2 * DEEP, YE - SUB
+    G = q_v.shape[1] // 3
+    row8 = lax.broadcasted_iota(jnp.int32, (SUB, Z), 0)
+    q = [[q_v[d, i:i + 1, :] for i in range(3 * G)] for d in range(5)]
+    side = [jnp.where(row8 < SUB // 2, hi, lo) for hi, lo in zip(q[4], q[3])]
+
+    def fill(x, q_in):
+        s = spread_over(reg_v[x, 0:Y], q_in, G)
+        t = spread_over(reg_v[x, Y:YE], side, G)
+        for c in range(3):
+            s_e[c, x, 0:Y] = s[c]
+            s_e[c, x, Y:YE] = t[c]
+
+    def fill_own(i, _):
+        fill(i + DEEP, q[0])
+        return 0
+
+    fill(DEEP - 1, q[1])
+    fill(DEEP + X, q[2])
+    looped(0, X, fill_own, 0)
+    faces = (kx, kym, kyp, kzm, kzp)
+    copies = []
+    parts = 4
+    step = X // parts
+
+    def plane(i, _):
+        x = i + DEEP
+        u = [s_e[c, x] for c in range(3)]
+        kk = k4[x, 0:Y] * (u[0] + u[1] + u[2])[0:Y]
+        for c in range(3):
+            av = ag_v[c, i] + (dg[x, 0:Y] * u[c][0:Y] + kk
+                               - stencil(u[c], s_e[c, x - 1], s_e[c, x + 1], faces, x, Y))
+            xb[c, i] = a * z_v[c, i] - b * (g_v[c, i] + u[c][0:Y])
+            rb[c, i] = r_v[c, i] - a * y_v[c, i] + b * av
+        return 0
+
+    for n in range(parts):
+        lax.fori_loop(n * step, (n + 1) * step, plane, 0, unroll=True)
+        for m, (src, dst) in enumerate(((xb, x_out), (rb, res_out))):
+            where = (slice(None), pl.ds(n * step, step))
+            copies.append(pltpu.make_async_copy(src.at[where], dst.at[where], sem.at[m, n]))
+            copies[-1].start()
+    for copy in copies:
+        copy.wait()
+
+
+def local_fast(nw, nn, right_side, occupancy, region, coarse_inverse):
+    _, X, Y, Z = right_side.shape
+    ncr, NC = coarse_inverse.shape
+    ND = nw * nn
+    f32, i32 = jnp.float32, jnp.int32
+    V = pltpu.VMEM
+    E, YE = X + 2 * DEEP, Y + SUB
+    field, ext, scal = (3, X, Y, Z), (3, E, YE, Z), (E, YE, Z)
+    ng = nw // group_of(nw)
+    DMA = pltpu.SemaphoreType.DMA
+    scratch = [
+        V(scal, i32), V(scal, i32), V(ext, f32), V(scal, f32), V(scal, f32), V(ext, f32), V(ext, f32),
+        V((2, ND // 2, ncr, NC), f32), V((8, ncr, NC), f32), V((2, ND, LANES), f32),
+        V((2, SUB, LANES), f32), V((2, ND, LANES), f32), V((3, SUB, LANES), f32), V((3, ND, LANES), f32),
+        DMA((4,)), DMA((3, 8)), DMA((3, 8)), DMA((8,)), DMA((8,)), DMA((5,)), DMA((5,)), DMA((2,)), DMA((2,)),
+        pltpu.SemaphoreType.REGULAR((ng + 2,)),
+    ]
+    outs = (V(field, f32),) * 5 + (V(scal, i32),) + (V(scal, f32),) * 7 + (V((5, ncr, LANES), f32), V((SUB, LANES), f32))
+    parts = pl.pallas_call(
+        functools.partial(kernel, nw, nn),
+        out_shape=outs,
+        in_specs=[pl.BlockSpec(memory_space=pltpu.HBM)] * 4,
+        out_specs=(pl.BlockSpec(memory_space=pltpu.VMEM),) * len(outs),
+        scratch_shapes=scratch,
+        compiler_params=pltpu.CompilerParams(collective_id=0, has_side_effects=True, vmem_limit_bytes=32 * 1024 * 1024),
+    )(*[pltpu.with_memory_space_constraint(a, pltpu.HBM) for a in (right_side, occupancy, region, coarse_inverse)])
+    return pl.pallas_call(
+        finish,
+        out_shape=(jax.ShapeDtypeStruct(field, f32),) * 2,
+        in_specs=[pl.BlockSpec(memory_space=pltpu.VMEM)] * len(outs),
+        out_specs=(pl.BlockSpec(memory_space=pltpu.HBM),) * 2,
+        scratch_shapes=[V(ext, f32), V(field, f32), V(field, f32), DMA((2, 4))],
+        compiler_params=pltpu.CompilerParams(vmem_limit_bytes=24 * 1024 * 1024),
+    )(*parts)
+
+
+def local(nw, nn, right_side, occupancy, region, coarse_inverse):
+    nc = coarse_inverse.shape[1]
+    run = local_fast if nw % 2 == 0 and nc * nc * 4 <= REPLICATED_BYTES else local_wide
+    return run(nw, nn, right_side, occupancy, region, coarse_inverse)
 
 
 def solution(mesh):

time: 25.3 us -> 25.3 us (level)
  no operation moved by 1% of the time
where the time goes in v2:
time: 25.3 us; the launch traced here: 25.1 us
  Pallas kernels  24.5 us (97%)
  between operations  0.64 us (3%)
    pallas_call x1, Pallas kernels, local_fast(): pl.pallas_call(functools.partial(kernel, nw, nn), out_shape=outs, in_spec...  23.2 us
    pallas_call x1, Pallas kernels, local_fast(): pl.pallas_call(finish, out_shape=(jax.ShapeDtypeStruct(field, f32),) * 2,...  1.26 us

profile of v2, /device:TPU:0, one launch (start us, length us, event | category | flops | bytes accessed | tf_op | source)
XLA Modules:
  0.0 25.1 jit_solution(16781030422484841268)
XLA Ops:
  0.6 23.2 %shard_map.59 = (f32[3,16,16,128]{3,2,1,0:T(8,128)S(1)}, f32[3,16,16,128]{3,2,1,0:T(8,128)S(1)}, f32[3,16,16,128]{3,2,1,0:T(8,128)S(1)}, f32[3,16,16,128]{3,2,1,...) custom-call(f32[3,16,16,128]{3,2,1,0:T(8,128)} %r_hbm.1, ...), custom_call_target="tpu_custom_call" | custom-call | tf_op jit(solution)/shard_map/pallas_call | solution.py:1072
  23.9 1.3 %shard_map.60 = (f32[3,16,16,128]{3,2,1,0:T(8,128)}, f32[3,16,16,128]{3,2,1,0:T(8,128)}) custom-call(f32[3,16,16,128]{3,2,1,0:T(8,128)S(1)} %get-tuple-element.17.z_v, f32[3,16,16,128]{3,2,1,0:T(8,128)S(1)} %get-tuple-element.18.g_v, f32[3,16,16,128]{3,2,1,0:T(8,128)S(1)} %get-tuple-element.19.r_v, f32[3,16,16,128]{3,2,1,0:T(8,128)S(1)} %get-tuple-element.20.y_v, ...), custom_call_target="tpu_custom_call" | custom-call | tf_op jit(solution)/shard_map/pallas_call | solution.py:1080

commit v3 on v2

--- a/solution.py
+++ b/solution.py
@@ -477,7 +477,7 @@
 def kernel(nw, nn, r_hbm, occ_hbm, reg_hbm, ci_hbm,
            z_o, g_o, r_o, y_o, ag_o, reg_o, k4, dg, kx, kym, kyp, kzm, kzp, q_o, sc_o,
            occ_e, reg_e, r_e, k_e, invd, z_e, g_e,
-           call, c_in, qpair, row_send, rows, ac_send, ac,
+           call, c_in, y_face, y_label, qpair, row_send, rows, ac_send, ac,
            load_sem, hs_send, hs_recv, hc_send, hc_recv, ag_send, ag_recv, cs_send, cs_recv, ready):
     E, YE, Z = occ_e.shape
     X, Y = E - 2 * DEEP, YE - SUB
@@ -488,11 +488,13 @@
     wi = lax.axis_index("wide")
     ni = lax.axis_index("narrow")
     me = wi * nn + ni
-    half, slot = lax.rem(wi, 2), (wi // 2) * nn + ni
     f32 = jnp.float32
-    GP = group_of(nw) * nn
+    GW = group_of(nw)
+    GP = GW * nn
     NG = ND // GP
     grp, pos = me // GP, lax.rem(me, GP)
+    half, place = lax.rem(wi, 2), (lax.rem(wi, GW) // 2) * nn + ni
+    slot = place * NG + grp
     own = pl.ds(DEEP, X)
 
     loads = [pltpu.make_async_copy(s, d, load_sem.at[i]) for i, (s, d) in enumerate((
@@ -511,24 +513,44 @@
         def _():
             pl.semaphore_wait(sem, count)
 
-    def greet(t, _):
-        pl.semaphore_signal(barrier, inc=1, device_id=at(t), device_id_type=MESH)
-        return 0
-
-    lax.fori_loop(me + 1, ND, greet, 0)
-
-    def kind_of(low, high):
-        apart = high // GP - low // GP
-        k = jnp.where(lax.rem(high, GP) == lax.rem(low, GP), apart, NG + 1)
-        aside = lax.rem(high, nn) - lax.rem(low, nn)
-        touch = jnp.logical_and(high // nn - low // nn == 1, jnp.logical_and(aside >= -1, aside <= 1))
-        k = jnp.where(touch, NG, k)
-        return jnp.where(apart == 0, 0, k)
-
-    def tell(i, _):
-        t = me - 1 - i
-        pl.semaphore_signal(ready.at[kind_of(t, me)], inc=1, device_id=at(t), device_id_type=MESH)
-        return 0
+    def column_of(group):
+        return (wi + (group - grp) * GW, ni)
+
+    at_low = jnp.logical_and(lax.rem(wi, GW) == 0, wi > 0)
+    at_high = jnp.logical_and(lax.rem(wi, GW) == GW - 1, wi < nw - 1)
+    aside = 1 + jnp.where(ni > 0, 1, 0) + jnp.where(ni < nn - 1, 1, 0)
+
+    def touching(ahead, signal):
+        @pl.when(at_high if ahead > 0 else at_low)
+        def _():
+            for b in (-1, 0, 1):
+                @pl.when(jnp.logical_and(ni + b >= 0, ni + b < nn))
+                def _():
+                    signal((wi + ahead, ni + b))
+
+    def say(sem):
+        return lambda device: pl.semaphore_signal(sem, inc=1, device_id=device, device_id_type=MESH)
+
+    for i in range(1, GP):
+        @pl.when(pos + i < GP)
+        def _():
+            say(barrier)(at(me + i))
+    touching(1, say(barrier))
+    for k in range(1, NG):
+        @pl.when(grp + k < NG)
+        def _():
+            say(barrier)(column_of(grp + k))
+
+    def tell():
+        for i in range(1, GP):
+            @pl.when(pos >= i)
+            def _():
+                say(ready.at[0])(at(me - i))
+        touching(-1, say(ready.at[NG]))
+        for k in range(1, NG):
+            @pl.when(grp >= k)
+            def _():
+                say(ready.at[k])(column_of(grp - k))
 
     has = []
     for a, b in AROUND:
@@ -557,8 +579,8 @@
                 ref[where] = jnp.full(v.shape, (-1, -1, 0)[n], v.dtype)
             c_in[d] = jnp.zeros((ncr, NC), f32)
 
-    wait_for(barrier, me)
-    lax.fori_loop(0, me, tell, 0)
+    wait_for(barrier, pos + grp + jnp.where(at_low, aside, 0))
+    tell()
 
     def fold(a):
         return jnp.sum(a.reshape(a.shape[0] // SUB, SUB, Z), axis=0)
@@ -601,12 +623,6 @@
             some = rows.at[p, pl.ds(0, count)]
             pltpu.make_async_copy(some, some, sem).wait()
 
-    def by_group(count, sem):
-        for n in range(NG):
-            @pl.when(grp == n)
-            def _():
-                rows_wait(0, count(n), sem)
-
     def each_peer(send):
         def body(i, _):
             send(lax.rem(me + i, ND))
@@ -625,12 +641,7 @@
         row_to(0, grp * GP + lax.rem(pos + i, GP), 0)
         return 0
 
-    def below(i, _):
-        row_to(0, grp * GP - 1 - i, 2)
-        return 0
-
     lax.fori_loop(1, GP, inside, 0, unroll=GP <= 64)
-    lax.fori_loop(0, grp * GP, below, 0)
 
     def halo(n, d):
         a, b = AROUND[d]
@@ -654,11 +665,8 @@
             send_sem=hs_send.at[n, d], recv_sem=hs_recv.at[n, d],
             device_id=(wi, ni), device_id_type=MESH).wait_recv()
 
-    beside = jnp.where(kind_of(me, me + nn) == NG, 1, 0)
-    touching = jnp.where(wi < nw - 1, beside * (
-        1 + jnp.where(ni > 0, 1, 0) + jnp.where(ni < nn - 1, 1, 0)), 0)
     loads[2].wait()
-    wait_for(ready.at[NG], touching)
+    wait_for(ready.at[NG], jnp.where(at_high, aside, 0))
     for n in range(3):
         for d in range(8):
             @pl.when(has[d])
@@ -670,55 +678,87 @@
         def _():
             halo_c(d).start()
 
-    rows_wait(0, GP - 1, ag_recv.at[0])
-    mine = rows.at[0, pl.ds(pl.multiple_of(grp * GP, GP), GP)]
-    for k in range(1, NG):
-        @pl.when(grp + k < NG)
-        def _():
-            if k * GP != nn:
-                pl.semaphore_wait(ready.at[k], 1)
-            pltpu.make_async_remote_copy(
-                src_ref=mine, dst_ref=mine, send_sem=ag_send.at[1], recv_sem=ag_recv.at[1],
-                device_id=at(me + k * GP), device_id_type=MESH).start()
-
-    rest = ND - 1 - me - (GP - 1 - pos) - touching
-    if GP != nn:
-        rest = rest - (NG - 1 - grp)
-    wait_for(ready.at[NG + 1], rest)
-
-    def send_c(i, _):
-        t = lax.rem(slot + i, NH)
+    def c_column(group):
         pltpu.make_async_remote_copy(
             src_ref=call.at[half, slot], dst_ref=call.at[half, slot],
             send_sem=cs_send.at[0], recv_sem=cs_recv.at[0],
-            device_id=((t // nn) * 2 + half, lax.rem(t, nn)), device_id_type=MESH).start()
-        return 0
-
-    lax.fori_loop(1, NH, send_c, 0)
-
-    for n in range(3):
-        for d in range(8):
-            @pl.when(has[d])
-            def _():
-                arrived(n, d)
-
-    lane_id = lax.broadcasted_iota(jnp.int32, (YE, Z), 1)
-
-    def stiffness(x, _):
-        o = occ_e[x]
-        k_e[x] = jnp.where(o < 0, 0.0, soft_stiff + (bone_stiff - soft_stiff) * o.astype(f32))
-        return 0
-
-    lax.fori_loop(0, E, stiffness, 0, unroll=True)
-
-    def pairs(acc, first, second, value):
+            device_id=column_of(group), device_id_type=MESH).start()
+
+    for k in range(1, NG):
+        @pl.when(grp >= k)
+        def _():
+            c_column(grp - k)
+
+    def stiff_of(o):
+        return jnp.where(o < 0, 0.0, soft_stiff + (bone_stiff - soft_stiff) * o.astype(f32))
+
+    n2 = G * G
+
+    def pairs(acc, first, seconds):
         out = list(acc)
         for g in range(G):
-            t = jnp.where(second == g, value, 0.0)
+            t = None
+            for label, value in seconds:
+                v = jnp.where(label == g, value, 0.0)
+                t = v if t is None else t + v
             for h in range(G):
                 out[h * G + g] = acc[h * G + g] + fold(jnp.where(first == h, t, 0.0))
         return out
 
+    row16 = lax.broadcasted_iota(jnp.int32, (Y, Z), 0)
+    lane16 = lax.broadcasted_iota(jnp.int32, (Y, Z), 1)
+
+    def own_pairs(i, carry):
+        x = i + DEEP
+        k, reg = stiff_of(occ_e[x, 0:Y]), reg_e[x, 0:Y]
+        later = jnp.minimum(i + 1, X - 1) + DEEP
+        kx_in = jnp.where(i < X - 1, 0.5 * (k + stiff_of(occ_e[later, 0:Y])), 0.0)
+        ky_in = jnp.where(row16 == Y - 1, 0.0, 0.5 * (k + pltpu.roll(k, Y - 1, 0)))
+        kz_in = jnp.where(lane16 == Z - 1, 0.0, 0.5 * (k + pltpu.roll(k, Z - 1, 1)))
+        acc = pairs(carry[:n2], reg, ((reg_e[later, 0:Y], kx_in), (pltpu.roll(reg, Y - 1, 0), ky_in),
+                                      (pltpu.roll(reg, Z - 1, 1), kz_in)))
+        sums = [carry[n2 + g] + fold(jnp.where(reg == g, 0.25 * k, 0.0)) for g in range(G)]
+        return tuple(acc) + tuple(sums)
+
+    own_acc = lax.fori_loop(0, X, own_pairs, zero_acc(n2 + G), unroll=2)
+    own_col = column(own_acc)
+
+    rows_wait(0, GP - 1, ag_recv.at[0])
+    mine = rows.at[0, pl.ds(pl.multiple_of(grp * GP, GP), GP)]
+
+    def across(group):
+        pltpu.make_async_remote_copy(
+            src_ref=mine, dst_ref=mine, send_sem=ag_send.at[1], recv_sem=ag_recv.at[1],
+            device_id=column_of(group), device_id_type=MESH).start()
+
+    for k in range(1, NG):
+        @pl.when(grp >= k)
+        def _():
+            across(grp - k)
+
+    for k in range(1, NG):
+        @pl.when(grp + k < NG)
+        def _():
+            pl.semaphore_wait(ready.at[k], 1)
+            across(grp + k)
+
+    for k in range(1, NG):
+        @pl.when(grp + k < NG)
+        def _():
+            c_column(grp + k)
+
+    for d in range(8):
+        @pl.when(has[d])
+        def _():
+            arrived(0, d)
+
+    lane_id = lax.broadcasted_iota(jnp.int32, (YE, Z), 1)
+
+    def stiffness(x, _):
+        k_e[x] = stiff_of(occ_e[x])
+        return 0
+
+    lax.fori_loop(0, E, stiffness, 0, unroll=True)
     row8 = lax.broadcasted_iota(jnp.int32, (SUB, Z), 0)
 
     def coefficients(x):
@@ -745,49 +785,36 @@
         dg[x] = d
         k4[x] = 0.25 * k
         invd[x] = inv
-        reg_o[x] = reg_e[x]
-        for c in range(3):
-            z_e[c, x] = r_e[c, x] * inv
-        return xp, yp, zp, d, 0.25 * k
-
-    def edge_plane(x):
+        return d
+
+    for x in (1, 2, DEEP + X, DEEP + X + 1):
         coefficients(x)
 
-    for x in (1, 2, DEEP + X, DEEP + X + 1):
-        edge_plane(x)
-
-    n2 = G * G
-
-    def inner(i, carry):
+    def inner(i, sums):
+        d = coefficients(i + DEEP)[0:Y]
+        reg = reg_e[i + DEEP, 0:Y]
+        return tuple(sums[g] + fold(jnp.where(reg == g, d, 0.0)) for g in range(G))
+
+    sum_acc = lax.fori_loop(0, X, inner, zero_acc(G), unroll=4)
+
+    for n in (2, 1):
+        for d in range(8):
+            @pl.when(has[d])
+            def _():
+                arrived(n, d)
+
+    def side_rows(i, _):
         x = i + DEEP
-        xp, yp, zp, d, kq = coefficients(x)
-        reg = reg_e[x]
-        r16 = reg[0:Y]
-        up = pltpu.roll(reg, YE - 1, 0)
-        inside_x = jnp.where(i < X - 1, xp[0:Y], 0.0)
-        to_x = xp[0:Y] - inside_x
-        last = yp[Y - SUB:Y]
-        inside_y = jnp.concatenate([yp[0:Y - SUB], jnp.where(row8 == SUB - 1, 0.0, last)], axis=0)
-        to_y = jnp.where(row8 == SUB - 1, last, 0.0)
-        ahead = pltpu.roll(r16, Z - 1, 1)
-        after = reg_e[x + 1, 0:Y]
-        own_acc, x_acc, y_acc = list(carry[:n2]), list(carry[n2:2 * n2]), list(carry[2 * n2:3 * n2])
-        sums = list(carry[3 * n2:])
-        for g in range(G):
-            t = jnp.where(after == g, inside_x, 0.0) + jnp.where(up[0:Y] == g, inside_y, 0.0)
-            t = t + jnp.where(ahead == g, zp[0:Y], 0.0)
-            for h in range(G):
-                own_acc[h * G + g] = own_acc[h * G + g] + fold(jnp.where(r16 == h, t, 0.0))
-            m = r16 == g
-            sums[g] = sums[g] + fold(jnp.where(m, d[0:Y], 0.0))
-            sums[G + g] = sums[G + g] + fold(jnp.where(m, kq[0:Y], 0.0))
-        y_acc = pairs(y_acc, r16[Y - SUB:Y], up[Y - SUB:Y], to_y)
-        return tuple(own_acc) + tuple(x_acc) + tuple(y_acc) + tuple(sums)
-
-    acc = lax.fori_loop(0, X, inner, zero_acc(3 * n2 + 2 * G), unroll=2)
+        y_face[pl.ds(i, 1), :] = kyp[x, Y - 1:Y, :]
+        y_label[0, pl.ds(i, 1), :] = reg_e[x, Y - 1:Y, :]
+        y_label[1, pl.ds(i, 1), :] = reg_e[x, Y:Y + 1, :]
+        return 0
+
+    looped(0, X, side_rows, 0)
     top = DEEP + X - 1
-    x_acc = pairs(zero_acc(n2), reg_e[top, 0:Y], reg_e[top + 1, 0:Y], kx[top + 1, 0:Y])
-    cols = [column(acc[:n2]), column(x_acc), column(acc[2 * n2:3 * n2]), column(acc[3 * n2:])]
+    x_acc = pairs(zero_acc(n2), reg_e[top, 0:Y], ((reg_e[top + 1, 0:Y], kx[top + 1, 0:Y]),))
+    y_acc = pairs(zero_acc(n2), y_label[0], ((y_label[1], y_face[...]),))
+    rim_col = column(tuple(x_acc) + tuple(y_acc) + tuple(sum_acc))
 
     lane = lax.broadcasted_iota(jnp.int32, (n2, LANES), 1)
     pair = lax.broadcasted_iota(jnp.int32, (n2, LANES), 0)
@@ -796,12 +823,14 @@
     def lanes_of(col, mask):
         return jnp.sum(jnp.where(mask, col, 0.0), axis=0, keepdims=True)
 
-    lane_g = lax.broadcasted_iota(jnp.int32, (2 * G, LANES), 1)
-    row_g = lax.broadcasted_iota(jnp.int32, (2 * G, LANES), 0)
-    start = jnp.where(row_g < G, 3 * (G + 1) * row_g, 3 * n2 + 9 * (row_g - G))
-    at_sum = jnp.logical_and(lane_g >= start, lane_g < start + jnp.where(row_g < G, 3, 9))
-    ac_rows = (lanes_of(cols[0], at_pair) * -2.0 + lanes_of(cols[3], at_sum),
-               lanes_of(cols[1], at_pair) * -2.0, lanes_of(cols[2], at_pair) * -2.0)
+    lane_g = lax.broadcasted_iota(jnp.int32, (G, LANES), 1)
+    row_g = lax.broadcasted_iota(jnp.int32, (G, LANES), 0)
+    diag_at, sum_at = 3 * (G + 1) * row_g, 3 * n2 + 9 * row_g
+    at_diag = jnp.logical_and(lane_g >= diag_at, lane_g < diag_at + 3)
+    at_sum = jnp.logical_and(lane_g >= sum_at, lane_g < sum_at + 9)
+    ac_rows = (lanes_of(own_col[0:n2], at_pair) * -2.0 + lanes_of(rim_col[2 * n2:], at_diag)
+               + lanes_of(own_col[n2:], at_sum),
+               lanes_of(rim_col[0:n2], at_pair) * -2.0, lanes_of(rim_col[n2:2 * n2], at_pair) * -2.0)
     for n in range(3):
         ac_send[n, 0:1, :] = ac_rows[n]
         ac[n, pl.ds(me, 1), :] = ac_rows[n]
@@ -809,10 +838,8 @@
     def send_ac(t):
         pltpu.make_async_remote_copy(
             src_ref=ac_send.at[:, pl.ds(0, 1)], dst_ref=ac.at[:, pl.ds(me, 1)],
-            send_sem=ag_send.at[4], recv_sem=ag_recv.at[4],
+            send_sem=ag_send.at[3], recv_sem=ag_recv.at[3],
             device_id=at(t), device_id_type=MESH).start()
-
-    each_peer(send_ac)
 
     def coarse_vector(block):
         tiles = []
@@ -841,14 +868,14 @@
     def as_list(q):
         return [q[i:i + 1, :] for i in range(ncr)]
 
-    by_group(lambda n: (NG - 1 - n) * GP, ag_recv.at[2])
-    by_group(lambda n: n * GP, ag_recv.at[1])
+    rows_wait(0, ND - GP, ag_recv.at[1])
     for d in range(8):
         @pl.when(has[d])
         def _():
             pltpu.make_async_remote_copy(
                 src_ref=c_in.at[d], dst_ref=c_in.at[d], send_sem=hc_send.at[d], recv_sem=hc_recv.at[d],
                 device_id=(wi, ni), device_id_type=MESH).wait_recv()
+    each_peer(send_ac)
     tiles = coarse_vector(rows[0])
     q = as_list(solve(tiles, call[half, slot]))
     qn = [as_list(solve(tiles, c_in[d])) for d in range(8)]
@@ -859,9 +886,20 @@
     def add_spread(x, q_in, q_out):
         s = spread_over(reg_e[x, 0:Y], q_in, G)
         t = spread_over(reg_e[x, Y:YE], q_out, G)
-        for c in range(3):
-            z_e[c, x, 0:Y] = z_e[c, x, 0:Y] + s[c]
-            z_e[c, x, Y:YE] = z_e[c, x, Y:YE] + t[c]
+        inv = invd[x]
+        reg_o[x] = reg_e[x]
+        for c in range(3):
+            z_e[c, x, 0:Y] = r_e[c, x, 0:Y] * inv[0:Y] + s[c]
+            z_e[c, x, Y:YE] = r_e[c, x, Y:YE] * inv[Y:YE] + t[c]
+
+    column_c = call.at[half, pl.ds(0, NG - 1)]
+    pltpu.make_async_copy(column_c, column_c, cs_recv.at[0]).wait()
+    for i in range(1, GP // 2):
+        p = lax.rem(place + i, GP // 2)
+        block = call.at[half, pl.ds(place * NG, NG)]
+        pltpu.make_async_remote_copy(
+            src_ref=block, dst_ref=block, send_sem=cs_send.at[1], recv_sem=cs_recv.at[1],
+            device_id=(grp * GW + (p // nn) * 2 + half, lax.rem(p, nn)), device_id_type=MESH).start()
 
     q_side = either(qn[3], qn[2])
 
@@ -923,18 +961,18 @@
 
     acc2 = lax.fori_loop(0, X, second, zero_acc(ncr + 1), unroll=4)
     make_row(1, tuple(acc1) + (acc2[ncr],) + tuple(acc2[:ncr]))
-    each_peer(lambda t: row_to(1, t, 3))
-
-    others = call.at[half, pl.ds(0, NH - 1)]
-    pltpu.make_async_copy(others, others, cs_recv.at[0]).wait()
+    each_peer(lambda t: row_to(1, t, 2))
+
+    others = call.at[half, pl.ds(0, NH - NG)]
+    pltpu.make_async_copy(others, others, cs_recv.at[1]).wait()
     swap = pltpu.make_async_remote_copy(
-        src_ref=call.at[half], dst_ref=call.at[half], send_sem=cs_send.at[1], recv_sem=cs_recv.at[1],
+        src_ref=call.at[half], dst_ref=call.at[half], send_sem=cs_send.at[2], recv_sem=cs_recv.at[2],
         device_id=(wi + 1 - 2 * half, ni), device_id_type=MESH)
     swap.start()
     some = ac.at[:, pl.ds(0, ND - 1)]
-    pltpu.make_async_copy(some, some, ag_recv.at[4]).wait()
+    pltpu.make_async_copy(some, some, ag_recv.at[3]).wait()
     swap.wait_recv()
-    rows_wait(1, ND - 1, ag_recv.at[3])
+    rows_wait(1, ND - 1, ag_recv.at[2])
 
     block = rows[1]
     b1 = coarse_vector(block)
@@ -957,7 +995,7 @@
     for w in range(nw):
         for n in range(nn):
             d = w * nn + n
-            q1 = solve(b1, call[w % 2, (w // 2) * nn + n])
+            q1 = solve(b1, call[w % 2, ((w % GW) // 2 * nn + n) * NG + w // GW])
             qpair[0, d:d + 1, :] = jnp.sum(jnp.where(m0, q1, 0.0), axis=0, keepdims=True)
             qpair[1, d:d + 1, :] = jnp.sum(jnp.where(m1, q1, 0.0), axis=0, keepdims=True)
             for t in range(d * ncr // LANES, (d * ncr + ncr - 1) // LANES + 1):
@@ -988,11 +1026,11 @@
         q_o[d + 1] = jnp.broadcast_to(solve(b1, c_in[d]), (ncr, LANES))
 
     rows_wait(0, GP - 1, ag_send.at[0])
-    by_group(lambda n: n * GP, ag_send.at[2])
-    by_group(lambda n: (NG - 1 - n) * GP, ag_send.at[1])
-    rows_wait(1, ND - 1, ag_send.at[3])
-    pltpu.make_async_copy(some, some, ag_send.at[4]).wait()
-    pltpu.make_async_copy(others, others, cs_send.at[0]).wait()
+    rows_wait(0, ND - GP, ag_send.at[1])
+    rows_wait(1, ND - 1, ag_send.at[2])
+    pltpu.make_async_copy(some, some, ag_send.at[3]).wait()
+    pltpu.make_async_copy(column_c, column_c, cs_send.at[0]).wait()
+    pltpu.make_async_copy(others, others, cs_send.at[1]).wait()
     swap.wait_send()
     for d in range(8):
         @pl.when(has[d])
@@ -1063,10 +1101,10 @@
     DMA = pltpu.SemaphoreType.DMA
     scratch = [
         V(scal, i32), V(scal, i32), V(ext, f32), V(scal, f32), V(scal, f32), V(ext, f32), V(ext, f32),
-        V((2, ND // 2, ncr, NC), f32), V((8, ncr, NC), f32), V((2, ND, LANES), f32),
+        V((2, ND // 2, ncr, NC), f32), V((8, ncr, NC), f32), V((X, Z), f32), V((2, X, Z), i32), V((2, ND, LANES), f32),
         V((2, SUB, LANES), f32), V((2, ND, LANES), f32), V((3, SUB, LANES), f32), V((3, ND, LANES), f32),
-        DMA((4,)), DMA((3, 8)), DMA((3, 8)), DMA((8,)), DMA((8,)), DMA((5,)), DMA((5,)), DMA((2,)), DMA((2,)),
-        pltpu.SemaphoreType.REGULAR((ng + 2,)),
+        DMA((4,)), DMA((3, 8)), DMA((3, 8)), DMA((8,)), DMA((8,)), DMA((4,)), DMA((4,)), DMA((3,)), DMA((3,)),
+        pltpu.SemaphoreType.REGULAR((ng + 1,)),
     ]
     outs = (V(field, f32),) * 5 + (V(scal, i32),) + (V(scal, f32),) * 7 + (V((5, ncr, LANES), f32), V((SUB, LANES), f32))
     parts = pl.pallas_call(
@@ -1089,7 +1127,7 @@
 
 def local(nw, nn, right_side, occupancy, region, coarse_inverse):
     nc = coarse_inverse.shape[1]
-    run = local_fast if nw % 2 == 0 and nc * nc * 4 <= REPLICATED_BYTES else local_wide
+    run = local_fast if group_of(nw) % 2 == 0 and nc * nc * 4 <= REPLICATED_BYTES else local_wide
     return run(nw, nn, right_side, occupancy, region, coarse_inverse)
 
 

time: 25.3 us -> 23.6 us (0.933)
  the two profiles are of different devices: /device:TPU:0 before, /device:TPU:1 now
where the time goes in v3:
time: 23.6 us; the launch traced here: 23.4 us
  Pallas kernels  22.8 us (97%)
  between operations  0.64 us (3%)
    pallas_call x1, Pallas kernels, local_fast(): pl.pallas_call(functools.partial(kernel, nw, nn), out_shape=outs, in_spec...  21.5 us
    pallas_call x1, Pallas kernels, local_fast(): pl.pallas_call(finish, out_shape=(jax.ShapeDtypeStruct(field, f32),) * 2,...  1.26 us

profile of v3, /device:TPU:1, one launch (start us, length us, event | category | flops | bytes accessed | tf_op | source)
XLA Modules:
  0.0 23.4 jit_solution(13086718932719451595)
XLA Ops:
  0.6 21.5 %shard_map.59 = (f32[3,16,16,128]{3,2,1,0:T(8,128)S(1)}, f32[3,16,16,128]{3,2,1,0:T(8,128)S(1)}, f32[3,16,16,128]{3,2,1,0:T(8,128)S(1)}, f32[3,16,16,128]{3,2,1,...) custom-call(f32[3,16,16,128]{3,2,1,0:T(8,128)} %r_hbm.1, ...), custom_call_target="tpu_custom_call" | custom-call | tf_op jit(solution)/shard_map/pallas_call | solution.py:1110
  22.2 1.3 %shard_map.60 = (f32[3,16,16,128]{3,2,1,0:T(8,128)}, f32[3,16,16,128]{3,2,1,0:T(8,128)}) custom-call(f32[3,16,16,128]{3,2,1,0:T(8,128)S(1)} %get-tuple-element.17.z_v, f32[3,16,16,128]{3,2,1,0:T(8,128)S(1)} %get-tuple-element.18.g_v, f32[3,16,16,128]{3,2,1,0:T(8,128)S(1)} %get-tuple-element.19.r_v, f32[3,16,16,128]{3,2,1,0:T(8,128)S(1)} %get-tuple-element.20.y_v, ...), custom_call_target="tpu_custom_call" | custom-call | tf_op jit(solution)/shard_map/pallas_call | solution.py:1118

commit v4 on v3

--- a/solution.py
+++ b/solution.py
@@ -477,7 +477,7 @@
 def kernel(nw, nn, r_hbm, occ_hbm, reg_hbm, ci_hbm,
            z_o, g_o, r_o, y_o, ag_o, reg_o, k4, dg, kx, kym, kyp, kzm, kzp, q_o, sc_o,
            occ_e, reg_e, r_e, k_e, invd, z_e, g_e,
-           call, c_in, y_face, y_label, qpair, row_send, rows, ac_send, ac,
+           call, c_in, y_face, y_label, qpair, row_send, rows,
            load_sem, hs_send, hs_recv, hc_send, hc_recv, ag_send, ag_recv, cs_send, cs_recv, ready):
     E, YE, Z = occ_e.shape
     X, Y = E - 2 * DEEP, YE - SUB
@@ -532,9 +532,7 @@
         return lambda device: pl.semaphore_signal(sem, inc=1, device_id=device, device_id_type=MESH)
 
     for i in range(1, GP):
-        @pl.when(pos + i < GP)
-        def _():
-            say(barrier)(at(me + i))
+        say(barrier)(at(grp * GP + lax.rem(pos + i, GP)))
     touching(1, say(barrier))
     for k in range(1, NG):
         @pl.when(grp + k < NG)
@@ -542,11 +540,7 @@
             say(barrier)(column_of(grp + k))
 
     def tell():
-        for i in range(1, GP):
-            @pl.when(pos >= i)
-            def _():
-                say(ready.at[0])(at(me - i))
-        touching(-1, say(ready.at[NG]))
+        touching(-1, say(ready.at[0]))
         for k in range(1, NG):
             @pl.when(grp >= k)
             def _():
@@ -579,7 +573,7 @@
                 ref[where] = jnp.full(v.shape, (-1, -1, 0)[n], v.dtype)
             c_in[d] = jnp.zeros((ncr, NC), f32)
 
-    wait_for(barrier, pos + grp + jnp.where(at_low, aside, 0))
+    wait_for(barrier, GP - 1 + grp + jnp.where(at_low, aside, 0))
     tell()
 
     def fold(a):
@@ -612,15 +606,15 @@
         row_send[p, 0:1, :] = row
         rows[p, pl.ds(me, 1), :] = row
 
-    def row_to(p, t, sem):
+    def rows_to(p, count, t, sem):
         pltpu.make_async_remote_copy(
-            src_ref=row_send.at[p, pl.ds(0, 1)], dst_ref=rows.at[p, pl.ds(me, 1)],
+            src_ref=row_send.at[pl.ds(p, count), pl.ds(0, 1)], dst_ref=rows.at[pl.ds(p, count), pl.ds(me, 1)],
             send_sem=ag_send.at[sem], recv_sem=ag_recv.at[sem],
             device_id=at(t), device_id_type=MESH).start()
 
-    def rows_wait(p, count, sem):
-        if count:
-            some = rows.at[p, pl.ds(0, count)]
+    def rows_wait(p, count, devices, sem):
+        if devices:
+            some = rows.at[pl.ds(p, count), pl.ds(0, devices)]
             pltpu.make_async_copy(some, some, sem).wait()
 
     def each_peer(send):
@@ -635,10 +629,8 @@
         a, reg_e[x + DEEP, 0:Y], [r_e[c, x + DEEP, 0:Y] for c in range(3)])), zero_acc(ncr))
     make_row(0, acc)
 
-    wait_for(ready.at[0], GP - 1 - pos)
-
     def inside(i, _):
-        row_to(0, grp * GP + lax.rem(pos + i, GP), 0)
+        rows_to(0, 1, grp * GP + lax.rem(pos + i, GP), 0)
         return 0
 
     lax.fori_loop(1, GP, inside, 0, unroll=GP <= 64)
@@ -666,17 +658,19 @@
             device_id=(wi, ni), device_id_type=MESH).wait_recv()
 
     loads[2].wait()
-    wait_for(ready.at[NG], jnp.where(at_high, aside, 0))
-    for n in range(3):
-        for d in range(8):
-            @pl.when(has[d])
-            def _():
-                halo(n, d).start()
     loads[3].wait()
-    for d in range(8):
-        @pl.when(has[d])
-        def _():
-            halo_c(d).start()
+
+    def halo_start(crossing):
+        for n in range(4):
+            for d, (a, b) in enumerate(AROUND):
+                if a > 0 or not crossing:
+                    now = at_high if crossing else jnp.logical_not(at_high)
+
+                    @pl.when(jnp.logical_and(has[d], now) if a > 0 else has[d])
+                    def _():
+                        (halo_c(d) if n == 3 else halo(n, d)).start()
+
+    halo_start(False)
 
     def c_column(group):
         pltpu.make_async_remote_copy(
@@ -688,6 +682,20 @@
         @pl.when(grp >= k)
         def _():
             c_column(grp - k)
+
+    def c_group(block, sem):
+        for i in range(1, GP // 2):
+            p = lax.rem(place + i, GP // 2)
+            pltpu.make_async_remote_copy(
+                src_ref=call.at[half, block], dst_ref=call.at[half, block],
+                send_sem=cs_send.at[sem], recv_sem=cs_recv.at[sem],
+                device_id=(grp * GW + (p // nn) * 2 + half, lax.rem(p, nn)), device_id_type=MESH).start()
+
+    def c_wait(blocks, sem):
+        some = call.at[half, pl.ds(0, blocks)]
+        pltpu.make_async_copy(some, some, sem).wait()
+
+    c_group(slot, 1)
 
     def stiff_of(o):
         return jnp.where(o < 0, 0.0, soft_stiff + (bone_stiff - soft_stiff) * o.astype(f32))
@@ -723,7 +731,15 @@
     own_acc = lax.fori_loop(0, X, own_pairs, zero_acc(n2 + G), unroll=2)
     own_col = column(own_acc)
 
-    rows_wait(0, GP - 1, ag_recv.at[0])
+    wait_for(ready.at[0], jnp.where(at_high, aside, 0))
+    halo_start(True)
+    for k in range(1, NG):
+        @pl.when(grp + k < NG)
+        def _():
+            pl.semaphore_wait(ready.at[k], 1)
+            c_column(grp + k)
+
+    rows_wait(0, 1, GP - 1, ag_recv.at[0])
     mine = rows.at[0, pl.ds(pl.multiple_of(grp * GP, GP), GP)]
 
     def across(group):
@@ -739,13 +755,7 @@
     for k in range(1, NG):
         @pl.when(grp + k < NG)
         def _():
-            pl.semaphore_wait(ready.at[k], 1)
             across(grp + k)
-
-    for k in range(1, NG):
-        @pl.when(grp + k < NG)
-        def _():
-            c_column(grp + k)
 
     for d in range(8):
         @pl.when(has[d])
@@ -832,14 +842,8 @@
                + lanes_of(own_col[n2:], at_sum),
                lanes_of(rim_col[0:n2], at_pair) * -2.0, lanes_of(rim_col[n2:2 * n2], at_pair) * -2.0)
     for n in range(3):
-        ac_send[n, 0:1, :] = ac_rows[n]
-        ac[n, pl.ds(me, 1), :] = ac_rows[n]
-
-    def send_ac(t):
-        pltpu.make_async_remote_copy(
-            src_ref=ac_send.at[:, pl.ds(0, 1)], dst_ref=ac.at[:, pl.ds(me, 1)],
-            send_sem=ag_send.at[3], recv_sem=ag_recv.at[3],
-            device_id=at(t), device_id_type=MESH).start()
+        row_send[n + 2, 0:1, :] = ac_rows[n]
+        rows[n + 2, pl.ds(me, 1), :] = ac_rows[n]
 
     def coarse_vector(block):
         tiles = []
@@ -868,14 +872,17 @@
     def as_list(q):
         return [q[i:i + 1, :] for i in range(ncr)]
 
-    rows_wait(0, ND - GP, ag_recv.at[1])
+    c_wait(NG - 1, cs_recv.at[0])
+    for k in range(1, NG):
+        c_group(place * NG + lax.rem(grp + k, NG), 2)
+
+    rows_wait(0, 1, ND - GP, ag_recv.at[1])
     for d in range(8):
         @pl.when(has[d])
         def _():
             pltpu.make_async_remote_copy(
                 src_ref=c_in.at[d], dst_ref=c_in.at[d], send_sem=hc_send.at[d], recv_sem=hc_recv.at[d],
                 device_id=(wi, ni), device_id_type=MESH).wait_recv()
-    each_peer(send_ac)
     tiles = coarse_vector(rows[0])
     q = as_list(solve(tiles, call[half, slot]))
     qn = [as_list(solve(tiles, c_in[d])) for d in range(8)]
@@ -891,15 +898,6 @@
         for c in range(3):
             z_e[c, x, 0:Y] = r_e[c, x, 0:Y] * inv[0:Y] + s[c]
             z_e[c, x, Y:YE] = r_e[c, x, Y:YE] * inv[Y:YE] + t[c]
-
-    column_c = call.at[half, pl.ds(0, NG - 1)]
-    pltpu.make_async_copy(column_c, column_c, cs_recv.at[0]).wait()
-    for i in range(1, GP // 2):
-        p = lax.rem(place + i, GP // 2)
-        block = call.at[half, pl.ds(place * NG, NG)]
-        pltpu.make_async_remote_copy(
-            src_ref=block, dst_ref=block, send_sem=cs_send.at[1], recv_sem=cs_recv.at[1],
-            device_id=(grp * GW + (p // nn) * 2 + half, lax.rem(p, nn)), device_id_type=MESH).start()
 
     q_side = either(qn[3], qn[2])
 
@@ -961,18 +959,16 @@
 
     acc2 = lax.fori_loop(0, X, second, zero_acc(ncr + 1), unroll=4)
     make_row(1, tuple(acc1) + (acc2[ncr],) + tuple(acc2[:ncr]))
-    each_peer(lambda t: row_to(1, t, 2))
-
-    others = call.at[half, pl.ds(0, NH - NG)]
-    pltpu.make_async_copy(others, others, cs_recv.at[1]).wait()
+    each_peer(lambda t: rows_to(1, 4, t, 2))
+
+    c_wait(GP // 2 - 1, cs_recv.at[1])
+    c_wait((GP // 2 - 1) * (NG - 1), cs_recv.at[2])
     swap = pltpu.make_async_remote_copy(
-        src_ref=call.at[half], dst_ref=call.at[half], send_sem=cs_send.at[2], recv_sem=cs_recv.at[2],
+        src_ref=call.at[half], dst_ref=call.at[half], send_sem=cs_send.at[3], recv_sem=cs_recv.at[3],
         device_id=(wi + 1 - 2 * half, ni), device_id_type=MESH)
     swap.start()
-    some = ac.at[:, pl.ds(0, ND - 1)]
-    pltpu.make_async_copy(some, some, ag_recv.at[3]).wait()
     swap.wait_recv()
-    rows_wait(1, ND - 1, ag_recv.at[2])
+    rows_wait(1, 4, ND - 1, ag_recv.at[2])
 
     block = rows[1]
     b1 = coarse_vector(block)
@@ -1004,7 +1000,7 @@
     dev = lax.broadcasted_iota(jnp.int32, (ND, LANES), 0)
     next_x = jnp.where(dev < ND - nn, pltpu.roll(second_q, ND - nn, 0), 0.0)
     next_y = jnp.where(dev < ND - 1, pltpu.roll(second_q, ND - 1, 0), 0.0)
-    energy = jnp.sum(first_q * (ac[0] * second_q + ac[1] * next_x + ac[2] * next_y), axis=0, keepdims=True)
+    energy = jnp.sum(first_q * (rows[2] * second_q + rows[3] * next_x + rows[4] * next_y), axis=0, keepdims=True)
     for t in range(len(b1)):
         energy = energy + 2.0 * h1[t] * lines[t]
     yv = b1[0] * lines[0]
@@ -1025,12 +1021,12 @@
     for d in range(4):
         q_o[d + 1] = jnp.broadcast_to(solve(b1, c_in[d]), (ncr, LANES))
 
-    rows_wait(0, GP - 1, ag_send.at[0])
-    rows_wait(0, ND - GP, ag_send.at[1])
-    rows_wait(1, ND - 1, ag_send.at[2])
-    pltpu.make_async_copy(some, some, ag_send.at[3]).wait()
-    pltpu.make_async_copy(column_c, column_c, cs_send.at[0]).wait()
-    pltpu.make_async_copy(others, others, cs_send.at[1]).wait()
+    rows_wait(0, 1, GP - 1, ag_send.at[0])
+    rows_wait(0, 1, ND - GP, ag_send.at[1])
+    rows_wait(1, 4, ND - 1, ag_send.at[2])
+    c_wait(NG - 1, cs_send.at[0])
+    c_wait(GP // 2 - 1, cs_send.at[1])
+    c_wait((GP // 2 - 1) * (NG - 1), cs_send.at[2])
     swap.wait_send()
     for d in range(8):
         @pl.when(has[d])
@@ -1102,9 +1098,9 @@
     scratch = [
         V(scal, i32), V(scal, i32), V(ext, f32), V(scal, f32), V(scal, f32), V(ext, f32), V(ext, f32),
         V((2, ND // 2, ncr, NC), f32), V((8, ncr, NC), f32), V((X, Z), f32), V((2, X, Z), i32), V((2, ND, LANES), f32),
-        V((2, SUB, LANES), f32), V((2, ND, LANES), f32), V((3, SUB, LANES), f32), V((3, ND, LANES), f32),
-        DMA((4,)), DMA((3, 8)), DMA((3, 8)), DMA((8,)), DMA((8,)), DMA((4,)), DMA((4,)), DMA((3,)), DMA((3,)),
-        pltpu.SemaphoreType.REGULAR((ng + 1,)),
+        V((5, SUB, LANES), f32), V((5, ND, LANES), f32),
+        DMA((4,)), DMA((3, 8)), DMA((3, 8)), DMA((8,)), DMA((8,)), DMA((3,)), DMA((3,)), DMA((4,)), DMA((4,)),
+        pltpu.SemaphoreType.REGULAR((ng,)),
     ]
     outs = (V(field, f32),) * 5 + (V(scal, i32),) + (V(scal, f32),) * 7 + (V((5, ncr, LANES), f32), V((SUB, LANES), f32))
     parts = pl.pallas_call(

time: 23.6 us -> 21.5 us (0.911)
  the two profiles are of different devices: /device:TPU:1 before, /device:TPU:0 now
where the time goes in v4:
time: 21.5 us; the launch traced here: 21.3 us
  Pallas kernels  20.7 us (96%)
  between operations  0.64 us (3%)
    pallas_call x1, Pallas kernels, local_fast(): pl.pallas_call(functools.partial(kernel, nw, nn), out_shape=outs, in_spec...  19.4 us
    pallas_call x1, Pallas kernels, local_fast(): pl.pallas_call(finish, out_shape=(jax.ShapeDtypeStruct(field, f32),) * 2,...  1.26 us

profile of v4, /device:TPU:0, one launch (start us, length us, event | category | flops | bytes accessed | tf_op | source)
XLA Modules:
  0.0 21.3 jit_solution(12658042748463018217)
XLA Ops:
  0.6 19.4 %shard_map.59 = (f32[3,16,16,128]{3,2,1,0:T(8,128)S(1)}, f32[3,16,16,128]{3,2,1,0:T(8,128)S(1)}, f32[3,16,16,128]{3,2,1,0:T(8,128)S(1)}, f32[3,16,16,128]{3,2,1,...) custom-call(f32[3,16,16,128]{3,2,1,0:T(8,128)} %r_hbm.1, ...), custom_call_target="tpu_custom_call" | custom-call | tf_op jit(solution)/shard_map/pallas_call | solution.py:1106
  20.0 1.3 %shard_map.60 = (f32[3,16,16,128]{3,2,1,0:T(8,128)}, f32[3,16,16,128]{3,2,1,0:T(8,128)}) custom-call(f32[3,16,16,128]{3,2,1,0:T(8,128)S(1)} %get-tuple-element.17.z_v, f32[3,16,16,128]{3,2,1,0:T(8,128)S(1)} %get-tuple-element.18.g_v, f32[3,16,16,128]{3,2,1,0:T(8,128)S(1)} %get-tuple-element.19.r_v, f32[3,16,16,128]{3,2,1,0:T(8,128)S(1)} %get-tuple-element.20.y_v, ...), custom_call_target="tpu_custom_call" | custom-call | tf_op jit(solution)/shard_map/pallas_call | solution.py:1114

commit v5 on v4

--- a/solution.py
+++ b/solution.py
@@ -534,13 +534,13 @@
     for i in range(1, GP):
         say(barrier)(at(grp * GP + lax.rem(pos + i, GP)))
     touching(1, say(barrier))
+    touching(-1, say(barrier))
     for k in range(1, NG):
         @pl.when(grp + k < NG)
         def _():
             say(barrier)(column_of(grp + k))
 
     def tell():
-        touching(-1, say(ready.at[0]))
         for k in range(1, NG):
             @pl.when(grp >= k)
             def _():
@@ -573,7 +573,7 @@
                 ref[where] = jnp.full(v.shape, (-1, -1, 0)[n], v.dtype)
             c_in[d] = jnp.zeros((ncr, NC), f32)
 
-    wait_for(barrier, GP - 1 + grp + jnp.where(at_low, aside, 0))
+    wait_for(barrier, GP - 1 + grp + jnp.where(at_low, aside, 0) + jnp.where(at_high, aside, 0))
     tell()
 
     def fold(a):
@@ -660,17 +660,11 @@
     loads[2].wait()
     loads[3].wait()
 
-    def halo_start(crossing):
-        for n in range(4):
-            for d, (a, b) in enumerate(AROUND):
-                if a > 0 or not crossing:
-                    now = at_high if crossing else jnp.logical_not(at_high)
-
-                    @pl.when(jnp.logical_and(has[d], now) if a > 0 else has[d])
-                    def _():
-                        (halo_c(d) if n == 3 else halo(n, d)).start()
-
-    halo_start(False)
+    for n in range(4):
+        for d in range(8):
+            @pl.when(has[d])
+            def _():
+                (halo_c(d) if n == 3 else halo(n, d)).start()
 
     def c_column(group):
         pltpu.make_async_remote_copy(
@@ -731,13 +725,14 @@
     own_acc = lax.fori_loop(0, X, own_pairs, zero_acc(n2 + G), unroll=2)
     own_col = column(own_acc)
 
-    wait_for(ready.at[0], jnp.where(at_high, aside, 0))
-    halo_start(True)
-    for k in range(1, NG):
+    def c_up(k):
         @pl.when(grp + k < NG)
         def _():
             pl.semaphore_wait(ready.at[k], 1)
             c_column(grp + k)
+
+    for k in range(1, NG):
+        c_up(k)
 
     rows_wait(0, 1, GP - 1, ag_recv.at[0])
     mine = rows.at[0, pl.ds(pl.multiple_of(grp * GP, GP), GP)]
@@ -967,6 +962,17 @@
         src_ref=call.at[half], dst_ref=call.at[half], send_sem=cs_send.at[3], recv_sem=cs_recv.at[3],
         device_id=(wi + 1 - 2 * half, ni), device_id_type=MESH)
     swap.start()
+    rows_wait(0, 1, GP - 1, ag_send.at[0])
+    rows_wait(0, 1, ND - GP, ag_send.at[1])
+    c_wait(NG - 1, cs_send.at[0])
+    c_wait(GP // 2 - 1, cs_send.at[1])
+    c_wait((GP // 2 - 1) * (NG - 1), cs_send.at[2])
+    for d in range(8):
+        @pl.when(has[d])
+        def _():
+            for n in range(3):
+                halo(n, d).wait_send()
+            halo_c(d).wait_send()
     swap.wait_recv()
     rows_wait(1, 4, ND - 1, ag_recv.at[2])
 
@@ -1021,19 +1027,8 @@
     for d in range(4):
         q_o[d + 1] = jnp.broadcast_to(solve(b1, c_in[d]), (ncr, LANES))
 
-    rows_wait(0, 1, GP - 1, ag_send.at[0])
-    rows_wait(0, 1, ND - GP, ag_send.at[1])
     rows_wait(1, 4, ND - 1, ag_send.at[2])
-    c_wait(NG - 1, cs_send.at[0])
-    c_wait(GP // 2 - 1, cs_send.at[1])
-    c_wait((GP // 2 - 1) * (NG - 1), cs_send.at[2])
     swap.wait_send()
-    for d in range(8):
-        @pl.when(has[d])
-        def _():
-            for n in range(3):
-                halo(n, d).wait_send()
-            halo_c(d).wait_send()
 
 
 def finish(z_v, g_v, r_v, y_v, ag_v, reg_v, k4, dg, kx, kym, kyp, kzm, kzp, q_v, sc_v, x_out, res_out, s_e, xb, rb, sem):

time: 21.5 us -> 21.2 us (0.986)
  Pallas kernels: 20.7 us -> 20.4 us
    pallas_call x1, Pallas kernels: 19.4 us -> 19.1 us  [local_fast(): pl.pallas_call(functools.partial(kernel, nw, nn), out_shape=outs, in_spec...]
where the time goes in v5:
time: 21.2 us; the launch traced here: 21 us
  Pallas kernels  20.4 us (96%)
  between operations  0.64 us (3%)
    pallas_call x1, Pallas kernels, local_fast(): pl.pallas_call(functools.partial(kernel, nw, nn), out_shape=outs, in_spec...  19.1 us
    pallas_call x1, Pallas kernels, local_fast(): pl.pallas_call(finish, out_shape=(jax.ShapeDtypeStruct(field, f32),) * 2,...  1.26 us

profile of v5, /device:TPU:0, one launch (start us, length us, event | category | flops | bytes accessed | tf_op | source)
XLA Modules:
  0.0 21.0 jit_solution(8815705121800544589)
XLA Ops:
  0.6 19.1 %shard_map.59 = (f32[3,16,16,128]{3,2,1,0:T(8,128)S(1)}, f32[3,16,16,128]{3,2,1,0:T(8,128)S(1)}, f32[3,16,16,128]{3,2,1,0:T(8,128)S(1)}, f32[3,16,16,128]{3,2,1,...) custom-call(f32[3,16,16,128]{3,2,1,0:T(8,128)} %r_hbm.1, ...), custom_call_target="tpu_custom_call" | custom-call | tf_op jit(solution)/shard_map/pallas_call | solution.py:1101
  19.8 1.3 %shard_map.60 = (f32[3,16,16,128]{3,2,1,0:T(8,128)}, f32[3,16,16,128]{3,2,1,0:T(8,128)}) custom-call(f32[3,16,16,128]{3,2,1,0:T(8,128)S(1)} %get-tuple-element.17.z_v, f32[3,16,16,128]{3,2,1,0:T(8,128)S(1)} %get-tuple-element.18.g_v, f32[3,16,16,128]{3,2,1,0:T(8,128)S(1)} %get-tuple-element.19.r_v, f32[3,16,16,128]{3,2,1,0:T(8,128)S(1)} %get-tuple-element.20.y_v, ...), custom_call_target="tpu_custom_call" | custom-call | tf_op jit(solution)/shard_map/pallas_call | solution.py:1109

commit v6 on v5

--- a/solution.py
+++ b/solution.py
@@ -477,8 +477,8 @@
 def kernel(nw, nn, r_hbm, occ_hbm, reg_hbm, ci_hbm,
            z_o, g_o, r_o, y_o, ag_o, reg_o, k4, dg, kx, kym, kyp, kzm, kzp, q_o, sc_o,
            occ_e, reg_e, r_e, k_e, invd, z_e, g_e,
-           call, c_in, y_face, y_label, qpair, row_send, rows,
-           load_sem, hs_send, hs_recv, hc_send, hc_recv, ag_send, ag_recv, cs_send, cs_recv, ready):
+           call, c_in, y_face, y_label, qpair, row_send, rows, sizes,
+           load_sem, send, recv, ready):
     E, YE, Z = occ_e.shape
     X, Y = E - 2 * DEEP, YE - SUB
     ncr, NC = c_in.shape[1:]
@@ -494,12 +494,12 @@
     NG = ND // GP
     grp, pos = me // GP, lax.rem(me, GP)
     half, place = lax.rem(wi, 2), (lax.rem(wi, GW) // 2) * nn + ni
-    slot = place * NG + grp
+    here = half * NH + place * NG + grp
     own = pl.ds(DEEP, X)
 
-    loads = [pltpu.make_async_copy(s, d, load_sem.at[i]) for i, (s, d) in enumerate((
-        (reg_hbm, reg_e.at[own, pl.ds(0, Y)]), (r_hbm, r_e.at[:, own, pl.ds(0, Y)]),
-        (occ_hbm, occ_e.at[own, pl.ds(0, Y)]), (ci_hbm, call.at[half, slot])))]
+    loads = [pltpu.make_async_copy(s, d, load_sem.at[i]) for s, d, i in (
+        (reg_hbm, reg_e.at[own, pl.ds(0, Y)], 0), (r_hbm, r_e.at[:, own, pl.ds(0, Y)], 0),
+        (occ_hbm, occ_e.at[own, pl.ds(0, Y)], 1), (ci_hbm, call.at[here], 2))]
     for l in loads:
         l.start()
 
@@ -544,7 +544,28 @@
         for k in range(1, NG):
             @pl.when(grp >= k)
             def _():
-                say(ready.at[k])(column_of(grp - k))
+                say(ready.at[k - 1])(column_of(grp - k))
+
+    def take(rows_of, sem):
+        some = sizes.at[pl.ds(0, rows_of)]
+        pltpu.make_async_copy(some, some, sem).wait()
+
+    def take_c(blocks, sem):
+        some = call.at[pl.ds(0, blocks)]
+        pltpu.make_async_copy(some, some, sem).wait()
+
+    def by_neighbours(wait):
+        nx = jnp.where(wi > 0, 1, 0) + jnp.where(wi < nw - 1, 1, 0)
+        ny = jnp.where(ni > 0, 1, 0) + jnp.where(ni < nn - 1, 1, 0)
+        for a in ((1,) if nw == 2 else (1, 2)):
+            for b in (range(min(nn, 2)) if nn == 1 else (1,) if nn == 2 else (1, 2)):
+                @pl.when(jnp.logical_and(nx == a, ny == b))
+                def _():
+                    wait(a, b)
+
+    def halo_rows(n, a, b):
+        deep, corner, count = ((DEEP, 2, 1), (2, 1, 1), (2, 1, 3))[n]
+        return count * (a * deep * Y + b * deep * X + a * b * corner * corner)
 
     has = []
     for a, b in AROUND:
@@ -606,16 +627,11 @@
         row_send[p, 0:1, :] = row
         rows[p, pl.ds(me, 1), :] = row
 
-    def rows_to(p, count, t, sem):
+    def rows_to(p, count, t, out, sem):
         pltpu.make_async_remote_copy(
             src_ref=row_send.at[pl.ds(p, count), pl.ds(0, 1)], dst_ref=rows.at[pl.ds(p, count), pl.ds(me, 1)],
-            send_sem=ag_send.at[sem], recv_sem=ag_recv.at[sem],
+            send_sem=send.at[out], recv_sem=recv.at[sem],
             device_id=at(t), device_id_type=MESH).start()
-
-    def rows_wait(p, count, devices, sem):
-        if devices:
-            some = rows.at[pl.ds(p, count), pl.ds(0, devices)]
-            pltpu.make_async_copy(some, some, sem).wait()
 
     def each_peer(send):
         def body(i, _):
@@ -623,14 +639,13 @@
             return 0
         lax.fori_loop(1, ND, body, 0, unroll=ND <= 64)
 
-    loads[0].wait()
-    loads[1].wait()
+    take(4 * X * Y, load_sem.at[0])
     acc = looped(0, X, lambda x, a: tuple(add_rc(
         a, reg_e[x + DEEP, 0:Y], [r_e[c, x + DEEP, 0:Y] for c in range(3)])), zero_acc(ncr))
     make_row(0, acc)
 
     def inside(i, _):
-        rows_to(0, 1, grp * GP + lax.rem(pos + i, GP), 0)
+        rows_to(0, 1, grp * GP + lax.rem(pos + i, GP), 0, 3)
         return 0
 
     lax.fori_loop(1, GP, inside, 0, unroll=GP <= 64)
@@ -640,22 +655,15 @@
         e = BACK[d]
         return pltpu.make_async_remote_copy(
             src_ref=fields[n].at[part(n, d, False)], dst_ref=fields[n].at[part(n, e, True)],
-            send_sem=hs_send.at[n, d], recv_sem=hs_recv.at[n, e],
+            send_sem=send.at[0], recv_sem=recv.at[min(n, 1)],
             device_id=(wi + a, ni + b), device_id_type=MESH)
 
     def halo_c(d):
         a, b = AROUND[d]
         return pltpu.make_async_remote_copy(
-            src_ref=call.at[half, slot], dst_ref=c_in.at[BACK[d]],
-            send_sem=hc_send.at[d], recv_sem=hc_recv.at[BACK[d]],
+            src_ref=call.at[here], dst_ref=c_in.at[BACK[d]],
+            send_sem=send.at[1], recv_sem=recv.at[2],
             device_id=(wi + a, ni + b), device_id_type=MESH)
-
-    def arrived(n, d):
-        where = part(n, d, True)
-        pltpu.make_async_remote_copy(
-            src_ref=fields[n].at[where], dst_ref=fields[n].at[where],
-            send_sem=hs_send.at[n, d], recv_sem=hs_recv.at[n, d],
-            device_id=(wi, ni), device_id_type=MESH).wait_recv()
 
     loads[2].wait()
     loads[3].wait()
@@ -668,8 +676,8 @@
 
     def c_column(group):
         pltpu.make_async_remote_copy(
-            src_ref=call.at[half, slot], dst_ref=call.at[half, slot],
-            send_sem=cs_send.at[0], recv_sem=cs_recv.at[0],
+            src_ref=call.at[here], dst_ref=call.at[here],
+            send_sem=send.at[2], recv_sem=recv.at[5],
             device_id=column_of(group), device_id_type=MESH).start()
 
     for k in range(1, NG):
@@ -677,19 +685,15 @@
         def _():
             c_column(grp - k)
 
-    def c_group(block, sem):
+    def c_group(block):
         for i in range(1, GP // 2):
             p = lax.rem(place + i, GP // 2)
             pltpu.make_async_remote_copy(
-                src_ref=call.at[half, block], dst_ref=call.at[half, block],
-                send_sem=cs_send.at[sem], recv_sem=cs_recv.at[sem],
+                src_ref=call.at[block], dst_ref=call.at[block],
+                send_sem=send.at[2], recv_sem=recv.at[6],
                 device_id=(grp * GW + (p // nn) * 2 + half, lax.rem(p, nn)), device_id_type=MESH).start()
 
-    def c_wait(blocks, sem):
-        some = call.at[half, pl.ds(0, blocks)]
-        pltpu.make_async_copy(some, some, sem).wait()
-
-    c_group(slot, 1)
+    c_group(here)
 
     def stiff_of(o):
         return jnp.where(o < 0, 0.0, soft_stiff + (bone_stiff - soft_stiff) * o.astype(f32))
@@ -728,18 +732,18 @@
     def c_up(k):
         @pl.when(grp + k < NG)
         def _():
-            pl.semaphore_wait(ready.at[k], 1)
+            pl.semaphore_wait(ready.at[k - 1], 1)
             c_column(grp + k)
 
     for k in range(1, NG):
         c_up(k)
 
-    rows_wait(0, 1, GP - 1, ag_recv.at[0])
+    take(GP - 1, recv.at[3])
     mine = rows.at[0, pl.ds(pl.multiple_of(grp * GP, GP), GP)]
 
     def across(group):
         pltpu.make_async_remote_copy(
-            src_ref=mine, dst_ref=mine, send_sem=ag_send.at[1], recv_sem=ag_recv.at[1],
+            src_ref=mine, dst_ref=mine, send_sem=send.at[0], recv_sem=recv.at[4],
             device_id=column_of(group), device_id_type=MESH).start()
 
     for k in range(1, NG):
@@ -752,10 +756,7 @@
         def _():
             across(grp + k)
 
-    for d in range(8):
-        @pl.when(has[d])
-        def _():
-            arrived(0, d)
+    by_neighbours(lambda a, b: take(halo_rows(0, a, b), recv.at[0]))
 
     lane_id = lax.broadcasted_iota(jnp.int32, (YE, Z), 1)
 
@@ -802,11 +803,7 @@
 
     sum_acc = lax.fori_loop(0, X, inner, zero_acc(G), unroll=4)
 
-    for n in (2, 1):
-        for d in range(8):
-            @pl.when(has[d])
-            def _():
-                arrived(n, d)
+    by_neighbours(lambda a, b: take(halo_rows(1, a, b) + halo_rows(2, a, b), recv.at[1]))
 
     def side_rows(i, _):
         x = i + DEEP
@@ -867,19 +864,14 @@
     def as_list(q):
         return [q[i:i + 1, :] for i in range(ncr)]
 
-    c_wait(NG - 1, cs_recv.at[0])
+    take_c(NG - 1, recv.at[5])
     for k in range(1, NG):
-        c_group(place * NG + lax.rem(grp + k, NG), 2)
-
-    rows_wait(0, 1, ND - GP, ag_recv.at[1])
-    for d in range(8):
-        @pl.when(has[d])
-        def _():
-            pltpu.make_async_remote_copy(
-                src_ref=c_in.at[d], dst_ref=c_in.at[d], send_sem=hc_send.at[d], recv_sem=hc_recv.at[d],
-                device_id=(wi, ni), device_id_type=MESH).wait_recv()
+        c_group(half * NH + place * NG + lax.rem(grp + k, NG))
+
+    take(ND - GP, recv.at[4])
+    by_neighbours(lambda a, b: take_c(a + b + a * b, recv.at[2]))
     tiles = coarse_vector(rows[0])
-    q = as_list(solve(tiles, call[half, slot]))
+    q = as_list(solve(tiles, call[here]))
     qn = [as_list(solve(tiles, c_in[d])) for d in range(8)]
 
     def either(hi, lo):
@@ -954,27 +946,19 @@
 
     acc2 = lax.fori_loop(0, X, second, zero_acc(ncr + 1), unroll=4)
     make_row(1, tuple(acc1) + (acc2[ncr],) + tuple(acc2[:ncr]))
-    each_peer(lambda t: rows_to(1, 4, t, 2))
-
-    c_wait(GP // 2 - 1, cs_recv.at[1])
-    c_wait((GP // 2 - 1) * (NG - 1), cs_recv.at[2])
+    each_peer(lambda t: rows_to(1, 4, t, 3, 7))
+
+    take_c((GP // 2 - 1) * NG, recv.at[6])
+    swap_half = call.at[pl.ds(half * NH, NH)]
     swap = pltpu.make_async_remote_copy(
-        src_ref=call.at[half], dst_ref=call.at[half], send_sem=cs_send.at[3], recv_sem=cs_recv.at[3],
+        src_ref=swap_half, dst_ref=swap_half, send_sem=send.at[2], recv_sem=recv.at[8],
         device_id=(wi + 1 - 2 * half, ni), device_id_type=MESH)
     swap.start()
-    rows_wait(0, 1, GP - 1, ag_send.at[0])
-    rows_wait(0, 1, ND - GP, ag_send.at[1])
-    c_wait(NG - 1, cs_send.at[0])
-    c_wait(GP // 2 - 1, cs_send.at[1])
-    c_wait((GP // 2 - 1) * (NG - 1), cs_send.at[2])
-    for d in range(8):
-        @pl.when(has[d])
-        def _():
-            for n in range(3):
-                halo(n, d).wait_send()
-            halo_c(d).wait_send()
+    by_neighbours(lambda a, b: take(
+        sum(halo_rows(n, a, b) for n in range(3)) + GP - 1 + (NG - 1) * GP, send.at[0]))
+    by_neighbours(lambda a, b: take_c(a + b + a * b, send.at[1]))
     swap.wait_recv()
-    rows_wait(1, 4, ND - 1, ag_recv.at[2])
+    take(4 * (ND - 1), recv.at[7])
 
     block = rows[1]
     b1 = coarse_vector(block)
@@ -997,7 +981,7 @@
     for w in range(nw):
         for n in range(nn):
             d = w * nn + n
-            q1 = solve(b1, call[w % 2, ((w % GW) // 2 * nn + n) * NG + w // GW])
+            q1 = solve(b1, call[w % 2 * NH + ((w % GW) // 2 * nn + n) * NG + w // GW])
             qpair[0, d:d + 1, :] = jnp.sum(jnp.where(m0, q1, 0.0), axis=0, keepdims=True)
             qpair[1, d:d + 1, :] = jnp.sum(jnp.where(m1, q1, 0.0), axis=0, keepdims=True)
             for t in range(d * ncr // LANES, (d * ncr + ncr - 1) // LANES + 1):
@@ -1023,12 +1007,12 @@
     a1b = alpha1 * beta
     for n, v in enumerate((alpha0 + a1b + alpha1, alpha1 * alpha0)):
         sc_o[n:n + 1, :] = jnp.broadcast_to(v, (1, LANES))
-    q_o[0] = jnp.broadcast_to(solve(b1, call[half, slot]), (ncr, LANES))
+    q_o[0] = jnp.broadcast_to(solve(b1, call[here]), (ncr, LANES))
     for d in range(4):
         q_o[d + 1] = jnp.broadcast_to(solve(b1, c_in[d]), (ncr, LANES))
 
-    rows_wait(1, 4, ND - 1, ag_send.at[2])
-    swap.wait_send()
+    take(4 * (ND - 1), send.at[3])
+    take_c(NG - 1 + (GP // 2 - 1) * NG + NH, send.at[2])
 
 
 def finish(z_v, g_v, r_v, y_v, ag_v, reg_v, k4, dg, kx, kym, kyp, kzm, kzp, q_v, sc_v, x_out, res_out, s_e, xb, rb, sem):
@@ -1092,10 +1076,10 @@
     DMA = pltpu.SemaphoreType.DMA
     scratch = [
         V(scal, i32), V(scal, i32), V(ext, f32), V(scal, f32), V(scal, f32), V(ext, f32), V(ext, f32),
-        V((2, ND // 2, ncr, NC), f32), V((8, ncr, NC), f32), V((X, Z), f32), V((2, X, Z), i32), V((2, ND, LANES), f32),
-        V((5, SUB, LANES), f32), V((5, ND, LANES), f32),
-        DMA((4,)), DMA((3, 8)), DMA((3, 8)), DMA((8,)), DMA((8,)), DMA((3,)), DMA((3,)), DMA((4,)), DMA((4,)),
-        pltpu.SemaphoreType.REGULAR((ng,)),
+        V((ND, ncr, NC), f32), V((8, ncr, NC), f32), V((X, Z), f32), V((2, X, Z), i32), V((2, ND, LANES), f32),
+        V((5, SUB, LANES), f32), V((5, ND, LANES), f32), V((4 * X * Y, LANES), f32),
+        DMA((3,)), DMA((4,)), DMA((9,)),
+        pltpu.SemaphoreType.REGULAR((ng - 1,)),
     ]
     outs = (V(field, f32),) * 5 + (V(scal, i32),) + (V(scal, f32),) * 7 + (V((5, ncr, LANES), f32), V((SUB, LANES), f32))
     parts = pl.pallas_call(

time: 21.2 us -> 20.6 us (0.972)
  Pallas kernels: 20.4 us -> 19.8 us
    pallas_call x1, Pallas kernels: 19.1 us -> 18.5 us  [local_fast(): pl.pallas_call(functools.partial(kernel, nw, nn), out_shape=outs, in_spec...]
where the time goes in v6:
time: 20.6 us; the launch traced here: 20.4 us
  Pallas kernels  19.8 us (96%)
  between operations  0.64 us (3%)
    pallas_call x1, Pallas kernels, local_fast(): pl.pallas_call(functools.partial(kernel, nw, nn), out_shape=outs, in_spec...  18.5 us
    pallas_call x1, Pallas kernels, local_fast(): pl.pallas_call(finish, out_shape=(jax.ShapeDtypeStruct(field, f32),) * 2,...  1.26 us

profile of v6, /device:TPU:0, one launch (start us, length us, event | category | flops | bytes accessed | tf_op | source)
XLA Modules:
  0.0 20.4 jit_solution(7083377181398363634)
XLA Ops:
  0.6 18.5 %shard_map.59 = (f32[3,16,16,128]{3,2,1,0:T(8,128)S(1)}, f32[3,16,16,128]{3,2,1,0:T(8,128)S(1)}, f32[3,16,16,128]{3,2,1,0:T(8,128)S(1)}, f32[3,16,16,128]{3,2,1,...) custom-call(f32[3,16,16,128]{3,2,1,0:T(8,128)} %r_hbm.1, ...), custom_call_target="tpu_custom_call" | custom-call | tf_op jit(solution)/shard_map/pallas_call | solution.py:1085
  19.2 1.3 %shard_map.60 = (f32[3,16,16,128]{3,2,1,0:T(8,128)}, f32[3,16,16,128]{3,2,1,0:T(8,128)}) custom-call(f32[3,16,16,128]{3,2,1,0:T(8,128)S(1)} %get-tuple-element.17.z_v, f32[3,16,16,128]{3,2,1,0:T(8,128)S(1)} %get-tuple-element.18.g_v, f32[3,16,16,128]{3,2,1,0:T(8,128)S(1)} %get-tuple-element.19.r_v, f32[3,16,16,128]{3,2,1,0:T(8,128)S(1)} %get-tuple-element.20.y_v, ...), custom_call_target="tpu_custom_call" | custom-call | tf_op jit(solution)/shard_map/pallas_call | solution.py:1093

commit v7 on v6

--- a/solution.py
+++ b/solution.py
@@ -453,34 +453,47 @@
     return max(d for d in range(1, n + 1) if n % d == 0 and d * d <= n)
 
 
-def spread_over(reg, q, G):
+def spread_over(reg, q, G, inside=False):
     masks = [reg == g for g in range(G)]
     out = []
     for c in range(3):
-        s = jnp.zeros(reg.shape, jnp.float32)
-        for g in range(G):
+        s = q[(G - 1) * 3 + c] if inside else jnp.where(masks[G - 1], q[(G - 1) * 3 + c], 0.0)
+        for g in range(G - 1):
             s = jnp.where(masks[g], q[g * 3 + c], s)
         out.append(s)
     return out
 
 
-def stencil(u, prev, after, faces, x, rows):
-    kx, kym, kyp, kzm, kzp = faces
-    YE, Z = u.shape
-    low, high = pltpu.roll(u, 1, 0)[0:rows], pltpu.roll(u, YE - 1, 0)[0:rows]
-    v = u[0:rows]
-    a = kx[x, 0:rows] * prev[0:rows] + kx[x + 1, 0:rows] * after[0:rows]
-    a = a + (kym[x, 0:rows] * low + kyp[x, 0:rows] * high)
-    return a + (kzm[x, 0:rows] * pltpu.roll(v, 1, 1) + kzp[x, 0:rows] * pltpu.roll(v, Z - 1, 1))
+def rows_from(low, count):
+    return pl.ds(SUB + low, count)
+
+
+def both_sides(ref, Y, *at):
+    row = lax.broadcasted_iota(jnp.int32, (SUB, LANES), 0)
+    return jnp.where(row < SUB // 2, ref[(*at, pl.ds(SUB + Y, SUB))], ref[(*at, pl.ds(0, SUB))])
+
+
+def apply(ref, coefficients, x, low, count):
+    kx, kyp, kzm, kzp, dg, k4 = coefficients
+    here, down, up = rows_from(low, count), rows_from(low - 1, count), rows_from(low + 1, count)
+    u = [ref[c, x, here] for c in range(3)]
+    kk = k4[x, here] * (u[0] + u[1] + u[2])
+    out = []
+    for c in range(3):
+        a = kx[x, here] * ref[c, x - 1, here] + kx[x + 1, here] * ref[c, x + 1, here]
+        a = a + (kyp[x, down] * ref[c, x, down] + kyp[x, here] * ref[c, x, up])
+        a = a + (kzm[x, here] * pltpu.roll(u[c], 1, 1) + kzp[x, here] * pltpu.roll(u[c], LANES - 1, 1))
+        out.append(dg[x, here] * u[c] + kk - a)
+    return u, out
 
 
 def kernel(nw, nn, r_hbm, occ_hbm, reg_hbm, ci_hbm,
-           z_o, g_o, r_o, y_o, ag_o, reg_o, k4, dg, kx, kym, kyp, kzm, kzp, q_o, sc_o,
-           occ_e, reg_e, r_e, k_e, invd, z_e, g_e,
+           z_e, g_e, y_e, r_o, ag_o, reg_o, k4, dg, kx, kyp, kzm, kzp, q_o, sc_o,
+           occ_e, reg_e, r_e, k_e, invd,
            call, c_in, y_face, y_label, qpair, row_send, rows, sizes,
            load_sem, send, recv, ready):
     E, YE, Z = occ_e.shape
-    X, Y = E - 2 * DEEP, YE - SUB
+    X, Y = E - 2 * DEEP, YE - 2 * SUB
     ncr, NC = c_in.shape[1:]
     G = ncr // 3
     ND = nw * nn
@@ -495,11 +508,11 @@
     grp, pos = me // GP, lax.rem(me, GP)
     half, place = lax.rem(wi, 2), (lax.rem(wi, GW) // 2) * nn + ni
     here = half * NH + place * NG + grp
-    own = pl.ds(DEEP, X)
+    own, inner_rows = pl.ds(DEEP, X), pl.ds(SUB, Y)
 
     loads = [pltpu.make_async_copy(s, d, load_sem.at[i]) for s, d, i in (
-        (reg_hbm, reg_e.at[own, pl.ds(0, Y)], 0), (r_hbm, r_e.at[:, own, pl.ds(0, Y)], 0),
-        (occ_hbm, occ_e.at[own, pl.ds(0, Y)], 1), (ci_hbm, call.at[here], 2))]
+        (reg_hbm, reg_e.at[own, inner_rows], 0), (r_hbm, r_e.at[:, own, inner_rows], 0),
+        (occ_hbm, occ_e.at[own, inner_rows], 1), (ci_hbm, call.at[here], 2))]
     for l in loads:
         l.start()
 
@@ -577,10 +590,10 @@
         deep = {0: DEEP, 1: 2, 2: 2}[arr] if a == 0 or b == 0 else {0: 2, 1: 1, 2: 1}[arr]
         if into:
             xs = {-1: (DEEP - deep, deep), 0: (DEEP, X), 1: (DEEP + X, deep)}[a]
-            ys = {-1: (YE - deep, deep), 0: (0, Y), 1: (Y, deep)}[b]
+            ys = {-1: (SUB - deep, deep), 0: (SUB, Y), 1: (SUB + Y, deep)}[b]
         else:
             xs = {-1: (DEEP, deep), 0: (DEEP, X), 1: (DEEP + X - deep, deep)}[a]
-            ys = {-1: (0, deep), 0: (0, Y), 1: (Y - deep, deep)}[b]
+            ys = {-1: (SUB, deep), 0: (SUB, Y), 1: (SUB + Y - deep, deep)}[b]
         xs, ys = pl.ds(*xs), pl.ds(*ys)
         return (slice(None), xs, ys) if arr == 2 else (xs, ys)
 
@@ -635,13 +648,13 @@
 
     def each_peer(send):
         def body(i, _):
-            send(lax.rem(me + i, ND))
+            send(i + jnp.where(i < me, 0, 1))
             return 0
-        lax.fori_loop(1, ND, body, 0, unroll=ND <= 64)
+        lax.fori_loop(0, ND - 1, body, 0, unroll=ND <= 64)
 
     take(4 * X * Y, load_sem.at[0])
     acc = looped(0, X, lambda x, a: tuple(add_rc(
-        a, reg_e[x + DEEP, 0:Y], [r_e[c, x + DEEP, 0:Y] for c in range(3)])), zero_acc(ncr))
+        a, reg_e[x + DEEP, inner_rows], [r_e[c, x + DEEP, inner_rows] for c in range(3)])), zero_acc(ncr))
     make_row(0, acc)
 
     def inside(i, _):
@@ -716,12 +729,12 @@
 
     def own_pairs(i, carry):
         x = i + DEEP
-        k, reg = stiff_of(occ_e[x, 0:Y]), reg_e[x, 0:Y]
+        k, reg = stiff_of(occ_e[x, inner_rows]), reg_e[x, inner_rows]
         later = jnp.minimum(i + 1, X - 1) + DEEP
-        kx_in = jnp.where(i < X - 1, 0.5 * (k + stiff_of(occ_e[later, 0:Y])), 0.0)
+        kx_in = jnp.where(i < X - 1, 0.5 * (k + stiff_of(occ_e[later, inner_rows])), 0.0)
         ky_in = jnp.where(row16 == Y - 1, 0.0, 0.5 * (k + pltpu.roll(k, Y - 1, 0)))
         kz_in = jnp.where(lane16 == Z - 1, 0.0, 0.5 * (k + pltpu.roll(k, Z - 1, 1)))
-        acc = pairs(carry[:n2], reg, ((reg_e[later, 0:Y], kx_in), (pltpu.roll(reg, Y - 1, 0), ky_in),
+        acc = pairs(carry[:n2], reg, ((reg_e[later, inner_rows], kx_in), (pltpu.roll(reg, Y - 1, 0), ky_in),
                                       (pltpu.roll(reg, Z - 1, 1), kz_in)))
         sums = [carry[n2 + g] + fold(jnp.where(reg == g, 0.25 * k, 0.0)) for g in range(G)]
         return tuple(acc) + tuple(sums)
@@ -758,7 +771,7 @@
 
     by_neighbours(lambda a, b: take(halo_rows(0, a, b), recv.at[0]))
 
-    lane_id = lax.broadcasted_iota(jnp.int32, (YE, Z), 1)
+    lane_id = lax.broadcasted_iota(jnp.int32, (Y + SUB, Z), 1)
 
     def stiffness(x, _):
         k_e[x] = stiff_of(occ_e[x])
@@ -768,37 +781,33 @@
     row8 = lax.broadcasted_iota(jnp.int32, (SUB, Z), 0)
 
     def coefficients(x):
-        k = k_e[x]
-        low, high = pltpu.roll(k, 1, 0), pltpu.roll(k, YE - 1, 0)
+        here = rows_from(-2, Y + SUB)
+        k = k_e[x, here]
+        low, high = k_e[x, rows_from(-3, Y + SUB)], k_e[x, rows_from(-1, Y + SUB)]
         back = jnp.where(lane_id == 0, 0.0, pltpu.roll(k, 1, 1))
         ahead = jnp.where(lane_id == Z - 1, 0.0, pltpu.roll(k, Z - 1, 1))
-        xm = 0.5 * (k + k_e[x - 1])
-        xp = 0.5 * (k + k_e[x + 1])
+        xm = 0.5 * (k + k_e[x - 1, here])
+        xp = 0.5 * (k + k_e[x + 1, here])
         ym = 0.5 * (k + low)
         yp = 0.5 * (k + high)
         zm = 0.5 * (k + back)
         zp = 0.5 * (k + ahead)
         diag = xm + xp + ym + yp + zm + zp + 0.5 * k
-        inv = jnp.where(k > 0.0, 1.0 / diag, 0.0)
-        zp = jnp.where(lane_id == Z - 1, 0.0, zp)
-        kx[x] = xm
-        kx[x + 1] = xp
-        kym[x] = ym
-        kyp[x] = yp
-        kzm[x] = jnp.where(lane_id == 0, 0.0, zm)
-        kzp[x] = zp
-        d = diag - 0.25 * k
-        dg[x] = d
-        k4[x] = 0.25 * k
-        invd[x] = inv
-        return d
+        kx[x, here] = xm
+        kx[x + 1, here] = xp
+        kyp[x, here] = yp
+        kzm[x, here] = jnp.where(lane_id == 0, 0.0, zm)
+        kzp[x, here] = jnp.where(lane_id == Z - 1, 0.0, zp)
+        dg[x, here] = diag - 0.25 * k
+        k4[x, here] = 0.25 * k
+        invd[x, here] = jnp.where(k > 0.0, 1.0 / diag, 0.0)
 
     for x in (1, 2, DEEP + X, DEEP + X + 1):
         coefficients(x)
 
     def inner(i, sums):
-        d = coefficients(i + DEEP)[0:Y]
-        reg = reg_e[i + DEEP, 0:Y]
+        coefficients(i + DEEP)
+        d, reg = dg[i + DEEP, inner_rows], reg_e[i + DEEP, inner_rows]
         return tuple(sums[g] + fold(jnp.where(reg == g, d, 0.0)) for g in range(G))
 
     sum_acc = lax.fori_loop(0, X, inner, zero_acc(G), unroll=4)
@@ -807,14 +816,14 @@
 
     def side_rows(i, _):
         x = i + DEEP
-        y_face[pl.ds(i, 1), :] = kyp[x, Y - 1:Y, :]
-        y_label[0, pl.ds(i, 1), :] = reg_e[x, Y - 1:Y, :]
-        y_label[1, pl.ds(i, 1), :] = reg_e[x, Y:Y + 1, :]
+        y_face[pl.ds(i, 1), :] = kyp[x, rows_from(Y - 1, 1), :]
+        y_label[0, pl.ds(i, 1), :] = reg_e[x, rows_from(Y - 1, 1), :]
+        y_label[1, pl.ds(i, 1), :] = reg_e[x, rows_from(Y, 1), :]
         return 0
 
     looped(0, X, side_rows, 0)
     top = DEEP + X - 1
-    x_acc = pairs(zero_acc(n2), reg_e[top, 0:Y], ((reg_e[top + 1, 0:Y], kx[top + 1, 0:Y]),))
+    x_acc = pairs(zero_acc(n2), reg_e[top, inner_rows], ((reg_e[top + 1, inner_rows], kx[top + 1, inner_rows]),))
     y_acc = pairs(zero_acc(n2), y_label[0], ((y_label[1], y_face[...]),))
     rim_col = column(tuple(x_acc) + tuple(y_acc) + tuple(sum_acc))
 
@@ -877,74 +886,72 @@
     def either(hi, lo):
         return [jnp.where(row8 < SUB // 2, a, b) for a, b in zip(hi, lo)]
 
-    def add_spread(x, q_in, q_out):
-        s = spread_over(reg_e[x, 0:Y], q_in, G)
-        t = spread_over(reg_e[x, Y:YE], q_out, G)
-        inv = invd[x]
-        reg_o[x] = reg_e[x]
-        for c in range(3):
-            z_e[c, x, 0:Y] = r_e[c, x, 0:Y] * inv[0:Y] + s[c]
-            z_e[c, x, Y:YE] = r_e[c, x, Y:YE] * inv[Y:YE] + t[c]
+    def add_spread(x, q_in, q_out, inside):
+        reg, inv = reg_e[x, inner_rows], invd[x, inner_rows]
+        s = spread_over(reg, q_in, G, inside)
+        reg_o[x, inner_rows] = reg
+        for c in range(3):
+            z_e[c, x, inner_rows] = r_e[c, x, inner_rows] * inv + s[c]
+        reg, inv = both_sides(reg_e, Y, x), both_sides(invd, Y, x)
+        s = spread_over(reg, q_out, G)
+        some = SUB // 2
+        reg_o[x, rows_from(Y, some)] = reg[0:some]
+        reg_o[x, rows_from(-some, some)] = reg[some:SUB]
+        for c in range(3):
+            z = both_sides(r_e, Y, c, x) * inv + s[c]
+            z_e[c, x, rows_from(Y, some)] = z[0:some]
+            z_e[c, x, rows_from(-some, some)] = z[some:SUB]
 
     q_side = either(qn[3], qn[2])
 
     def spread_own(i, _):
-        add_spread(i + DEEP, q, q_side)
+        add_spread(i + DEEP, q, q_side, True)
         return 0
 
     looped(0, X, spread_own, 0)
     q_low, q_high = either(qn[5], qn[4]), either(qn[7], qn[6])
     for x in (1, 2):
-        add_spread(x, qn[0], q_low)
+        add_spread(x, qn[0], q_low, False)
     for x in (DEEP + X, DEEP + X + 1):
-        add_spread(x, qn[1], q_high)
-
-    faces = (kx, kym, kyp, kzm, kzp)
-
-    def apply(ref, x, rows_):
-        u = [ref[c, x] for c in range(3)]
-        kk = k4[x, 0:rows_] * (u[0] + u[1] + u[2])[0:rows_]
-        return u, [dg[x, 0:rows_] * u[c][0:rows_] + kk
-                   - stencil(u[c], ref[c, x - 1], ref[c, x + 1], faces, x, rows_) for c in range(3)]
+        add_spread(x, qn[1], q_high, False)
+
+    faces = (kx, kyp, kzm, kzp, dg, k4)
 
     def dots(a, b):
         return fold(a[0] * b[0] + a[1] * b[1] + a[2] * b[2])
 
-    for x in (DEEP - 1, DEEP + X):
-        _, a = apply(z_e, x, YE)
-        for c in range(3):
-            g_e[c, x] = a[c] * invd[x]
-
-    def first(i, carry):
-        x = i + DEEP
-        u, a = apply(z_e, x, YE)
-        w = []
-        for c in range(3):
-            w.append(a[c] * invd[x])
-            g_e[c, x] = w[c]
-        y = [a[c][0:Y] for c in range(3)]
-        u = [u[c][0:Y] for c in range(3)]
-        w = [w[c][0:Y] for c in range(3)]
-        r = [r_e[c, x, 0:Y] for c in range(3)]
-        for c in range(3):
-            y_o[c, i] = y[c]
-            z_o[c, i] = u[c]
-            g_o[c, i] = w[c]
-            r_o[c, i] = r[c]
-        acc = add_rc(carry[:ncr], reg_e[x, 0:Y], y)
-        return tuple(acc) + (carry[ncr] + dots(r, u), carry[ncr + 1] + dots(y, u), carry[ncr + 2] + dots(y, w))
-
-    acc1 = lax.fori_loop(0, X, first, zero_acc(ncr + 3), unroll=4)
+    def first(i, _):
+        x, some = i + DEEP - 1, rows_from(-1, Y + SUB)
+        _, a = apply(z_e, faces, x, -1, Y + SUB)
+        for c in range(3):
+            y_e[c, x, some] = a[c]
+            g_e[c, x, some] = a[c] * invd[x, some]
+        return 0
+
+    lax.fori_loop(0, X + 2, first, 0, unroll=(X + 2) // 2)
+
+    def own_of(ref, x):
+        return [ref[c, x, inner_rows] for c in range(3)]
 
     def second(i, carry):
         x = i + DEEP
-        w, a = apply(g_e, x, Y)
+        w, a = apply(g_e, faces, x, 0, Y)
         for c in range(3):
             ag_o[c, i] = a[c]
-        acc = add_rc(carry[:ncr], reg_e[x, 0:Y], a)
-        return tuple(acc) + (carry[ncr] + dots([v[0:Y] for v in w], a),)
-
-    acc2 = lax.fori_loop(0, X, second, zero_acc(ncr + 1), unroll=4)
+        acc = add_rc(carry[:ncr], reg_e[x, inner_rows], a)
+        return tuple(acc) + (carry[ncr] + dots(w, a),)
+
+    acc2 = lax.fori_loop(0, X, second, zero_acc(ncr + 1), unroll=8)
+
+    def third(i, carry):
+        x = i + DEEP
+        r, z, y, w = own_of(r_e, x), own_of(z_e, x), own_of(y_e, x), own_of(g_e, x)
+        for c in range(3):
+            r_o[c, i] = r[c]
+        acc = add_rc(carry[:ncr], reg_e[x, inner_rows], y)
+        return tuple(acc) + (carry[ncr] + dots(r, z), carry[ncr + 1] + dots(y, z), carry[ncr + 2] + dots(y, w))
+
+    acc1 = lax.fori_loop(0, X, third, zero_acc(ncr + 3), unroll=8)
     make_row(1, tuple(acc1) + (acc2[ncr],) + tuple(acc2[:ncr]))
     each_peer(lambda t: rows_to(1, 4, t, 3, 7))
 
@@ -977,7 +984,7 @@
                 k = 3 * n2 + h * 9 + c * 3 + e
                 m0 = jnp.logical_or(m0, (ll == k) & (rr == h * 3 + c))
                 m1 = jnp.logical_or(m1, (ll == k) & (rr == h * 3 + e))
-    lines = [jnp.zeros((1, LANES), f32) for _ in b1]
+    lines = [jnp.zeros((ncr, LANES), f32) for _ in b1]
     for w in range(nw):
         for n in range(nn):
             d = w * nn + n
@@ -985,7 +992,8 @@
             qpair[0, d:d + 1, :] = jnp.sum(jnp.where(m0, q1, 0.0), axis=0, keepdims=True)
             qpair[1, d:d + 1, :] = jnp.sum(jnp.where(m1, q1, 0.0), axis=0, keepdims=True)
             for t in range(d * ncr // LANES, (d * ncr + ncr - 1) // LANES + 1):
-                lines[t] = lines[t] + jnp.sum(jnp.where(ll + LANES * t == rr + d * ncr, q1, 0.0), axis=0, keepdims=True)
+                lines[t] = jnp.where(ll + LANES * t == rr + d * ncr, q1, lines[t])
+    lines = [jnp.sum(v, axis=0, keepdims=True) for v in lines]
     first_q, second_q = qpair[0], qpair[1]
     dev = lax.broadcasted_iota(jnp.int32, (ND, LANES), 0)
     next_x = jnp.where(dev < ND - nn, pltpu.roll(second_q, ND - nn, 0), 0.0)
@@ -1015,53 +1023,55 @@
     take_c(NG - 1 + (GP // 2 - 1) * NG + NH, send.at[2])
 
 
-def finish(z_v, g_v, r_v, y_v, ag_v, reg_v, k4, dg, kx, kym, kyp, kzm, kzp, q_v, sc_v, x_out, res_out, s_e, xb, rb, sem):
+def finish(z_v, g_v, y_v, r_v, ag_v, reg_v, k4, dg, kx, kyp, kzm, kzp, q_v, sc_v, x_out, res_out, s_e, xb, rb, sem):
     a, b = sc_v[0:1, 0:1], sc_v[1:2, 0:1]
     E, YE, Z = reg_v.shape
-    X, Y = E - 2 * DEEP, YE - SUB
+    X, Y = E - 2 * DEEP, YE - 2 * SUB
     G = q_v.shape[1] // 3
+    own = pl.ds(SUB, Y)
     row8 = lax.broadcasted_iota(jnp.int32, (SUB, Z), 0)
     q = [[q_v[d, i:i + 1, :] for i in range(3 * G)] for d in range(5)]
     side = [jnp.where(row8 < SUB // 2, hi, lo) for hi, lo in zip(q[4], q[3])]
 
-    def fill(x, q_in):
-        s = spread_over(reg_v[x, 0:Y], q_in, G)
-        t = spread_over(reg_v[x, Y:YE], side, G)
-        for c in range(3):
-            s_e[c, x, 0:Y] = s[c]
-            s_e[c, x, Y:YE] = t[c]
+    def fill(x, q_in, inside):
+        s = spread_over(reg_v[x, own], q_in, G, inside)
+        for c in range(3):
+            s_e[c, x, own] = s[c]
+
+    def fill_sides(x):
+        s = spread_over(both_sides(reg_v, Y, x), side, G)
+        some = SUB // 2
+        for c in range(3):
+            s_e[c, x, rows_from(Y, some)] = s[c][0:some]
+            s_e[c, x, rows_from(-some, some)] = s[c][some:SUB]
 
     def fill_own(i, _):
-        fill(i + DEEP, q[0])
-        return 0
-
-    fill(DEEP - 1, q[1])
-    fill(DEEP + X, q[2])
+        fill(i + DEEP, q[0], True)
+        fill_sides(i + DEEP)
+        return 0
+
+    fill(DEEP - 1, q[1], False)
+    fill(DEEP + X, q[2], False)
     looped(0, X, fill_own, 0)
-    faces = (kx, kym, kyp, kzm, kzp)
-    copies = []
+    faces = (kx, kyp, kzm, kzp, dg, k4)
     parts = 4
     step = X // parts
 
     def plane(i, _):
         x = i + DEEP
-        u = [s_e[c, x] for c in range(3)]
-        kk = k4[x, 0:Y] * (u[0] + u[1] + u[2])[0:Y]
-        for c in range(3):
-            av = ag_v[c, i] + (dg[x, 0:Y] * u[c][0:Y] + kk
-                               - stencil(u[c], s_e[c, x - 1], s_e[c, x + 1], faces, x, Y))
-            xb[c, i] = a * z_v[c, i] - b * (g_v[c, i] + u[c][0:Y])
-            rb[c, i] = r_v[c, i] - a * y_v[c, i] + b * av
+        u, w = apply(s_e, faces, x, 0, Y)
+        for c in range(3):
+            xb[c, i] = a * z_v[c, x, own] - b * (g_v[c, x, own] + u[c])
+            rb[c, i] = r_v[c, i] - a * y_v[c, x, own] + b * (ag_v[c, i] + w[c])
         return 0
 
     for n in range(parts):
         lax.fori_loop(n * step, (n + 1) * step, plane, 0, unroll=True)
         for m, (src, dst) in enumerate(((xb, x_out), (rb, res_out))):
             where = (slice(None), pl.ds(n * step, step))
-            copies.append(pltpu.make_async_copy(src.at[where], dst.at[where], sem.at[m, n]))
-            copies[-1].start()
-    for copy in copies:
-        copy.wait()
+            pltpu.make_async_copy(src.at[where], dst.at[where], sem.at[m]).start()
+    pltpu.make_async_copy(xb, x_out, sem.at[0]).wait()
+    pltpu.make_async_copy(rb, res_out, sem.at[1]).wait()
 
 
 def local_fast(nw, nn, right_side, occupancy, region, coarse_inverse):
@@ -1070,18 +1080,18 @@
     ND = nw * nn
     f32, i32 = jnp.float32, jnp.int32
     V = pltpu.VMEM
-    E, YE = X + 2 * DEEP, Y + SUB
+    E, YE = X + 2 * DEEP, Y + 2 * SUB
     field, ext, scal = (3, X, Y, Z), (3, E, YE, Z), (E, YE, Z)
     ng = nw // group_of(nw)
     DMA = pltpu.SemaphoreType.DMA
     scratch = [
-        V(scal, i32), V(scal, i32), V(ext, f32), V(scal, f32), V(scal, f32), V(ext, f32), V(ext, f32),
+        V(scal, i32), V(scal, i32), V(ext, f32), V(scal, f32), V(scal, f32),
         V((ND, ncr, NC), f32), V((8, ncr, NC), f32), V((X, Z), f32), V((2, X, Z), i32), V((2, ND, LANES), f32),
         V((5, SUB, LANES), f32), V((5, ND, LANES), f32), V((4 * X * Y, LANES), f32),
         DMA((3,)), DMA((4,)), DMA((9,)),
         pltpu.SemaphoreType.REGULAR((ng - 1,)),
     ]
-    outs = (V(field, f32),) * 5 + (V(scal, i32),) + (V(scal, f32),) * 7 + (V((5, ncr, LANES), f32), V((SUB, LANES), f32))
+    outs = (V(ext, f32),) * 3 + (V(field, f32),) * 2 + (V(scal, i32),) + (V(scal, f32),) * 6 + (V((5, ncr, LANES), f32), V((SUB, LANES), f32))
     parts = pl.pallas_call(
         functools.partial(kernel, nw, nn),
         out_shape=outs,
@@ -1095,7 +1105,7 @@
         out_shape=(jax.ShapeDtypeStruct(field, f32),) * 2,
         in_specs=[pl.BlockSpec(memory_space=pltpu.VMEM)] * len(outs),
         out_specs=(pl.BlockSpec(memory_space=pltpu.HBM),) * 2,
-        scratch_shapes=[V(ext, f32), V(field, f32), V(field, f32), DMA((2, 4))],
+        scratch_shapes=[V(ext, f32), V(field, f32), V(field, f32), DMA((2,))],
         compiler_params=pltpu.CompilerParams(vmem_limit_bytes=24 * 1024 * 1024),
     )(*parts)
 

time: 20.6 us -> 20.3 us (0.985)
  Pallas kernels: 19.8 us -> 19.5 us
    pallas_call x1, Pallas kernels: 18.5 us -> 18.3 us  [local_fast(): pl.pallas_call(functools.partial(kernel, nw, nn), out_shape=outs, in_spec...]
where the time goes in v7:
time: 20.3 us; the launch traced here: 20.2 us
  Pallas kernels  19.5 us (96%)
  between operations  0.64 us (3%)
    pallas_call x1, Pallas kernels, local_fast(): pl.pallas_call(functools.partial(kernel, nw, nn), out_shape=outs, in_spec...  18.3 us
    pallas_call x1, Pallas kernels, local_fast(): pl.pallas_call(finish, out_shape=(jax.ShapeDtypeStruct(field, f32),) * 2,...  1.2 us

profile of v7, /device:TPU:0, one launch (start us, length us, event | category | flops | bytes accessed | tf_op | source)
XLA Modules:
  0.0 20.2 jit_solution(14808816929972731423)
XLA Ops:
  0.6 18.3 %shard_map.59 = (f32[3,22,32,128]{3,2,1,0:T(8,128)S(1)}, f32[3,22,32,128]{3,2,1,0:T(8,128)S(1)}, f32[3,22,32,128]{3,2,1,0:T(8,128)S(1)}, f32[3,16,16,128]{3,2,1,...) custom-call(f32[3,16,16,128]{3,2,1,0:T(8,128)} %r_hbm.1, ...), custom_call_target="tpu_custom_call" | custom-call | tf_op jit(solution)/shard_map/pallas_call | solution.py:1095
  19.0 1.2 %shard_map.60 = (f32[3,16,16,128]{3,2,1,0:T(8,128)}, f32[3,16,16,128]{3,2,1,0:T(8,128)}) custom-call(f32[3,22,32,128]{3,2,1,0:T(8,128)S(1)} %get-tuple-element.16.z_v, f32[3,22,32,128]{3,2,1,0:T(8,128)S(1)} %get-tuple-element.17.g_v, f32[3,22,32,128]{3,2,1,0:T(8,128)S(1)} %get-tuple-element.18.y_v, f32[3,16,16,128]{3,2,1,0:T(8,128)S(1)} %get-tuple-element.19.r_v, ...), custom_call_target="tpu_custom_call" | custom-call | tf_op jit(solution)/shard_map/pallas_call | solution.py:1103

commit v8 on v7

--- a/solution.py
+++ b/solution.py
@@ -681,11 +681,26 @@
     loads[2].wait()
     loads[3].wait()
 
-    for n in range(4):
+    for n in range(3):
         for d in range(8):
             @pl.when(has[d])
             def _():
-                (halo_c(d) if n == 3 else halo(n, d)).start()
+                halo(n, d).start()
+
+    def c_group(block, sem):
+        for i in range(1, GP // 2):
+            p = lax.rem(place + i, GP // 2)
+            pltpu.make_async_remote_copy(
+                src_ref=call.at[block], dst_ref=call.at[block],
+                send_sem=send.at[2], recv_sem=recv.at[sem],
+                device_id=(grp * GW + (p // nn) * 2 + half, lax.rem(p, nn)), device_id_type=MESH).start()
+
+    c_group(here, 9)
+    for d in range(8):
+        if AROUND[d][0]:
+            @pl.when(has[d])
+            def _():
+                halo_c(d).start()
 
     def c_column(group):
         pltpu.make_async_remote_copy(
@@ -697,16 +712,6 @@
         @pl.when(grp >= k)
         def _():
             c_column(grp - k)
-
-    def c_group(block):
-        for i in range(1, GP // 2):
-            p = lax.rem(place + i, GP // 2)
-            pltpu.make_async_remote_copy(
-                src_ref=call.at[block], dst_ref=call.at[block],
-                send_sem=send.at[2], recv_sem=recv.at[6],
-                device_id=(grp * GW + (p // nn) * 2 + half, lax.rem(p, nn)), device_id_type=MESH).start()
-
-    c_group(here)
 
     def stiff_of(o):
         return jnp.where(o < 0, 0.0, soft_stiff + (bone_stiff - soft_stiff) * o.astype(f32))
@@ -870,18 +875,23 @@
             s = s + block[:, t * LANES:(t + 1) * LANES] * tiles[t]
         return jnp.sum(s, axis=1, keepdims=True)
 
+    def rows_of(d):
+        a, b = AROUND[d]
+        return c_in[d] if a else call[here + jnp.where(has[d], b * NG, 0)]
+
     def as_list(q):
         return [q[i:i + 1, :] for i in range(ncr)]
 
     take_c(NG - 1, recv.at[5])
     for k in range(1, NG):
-        c_group(half * NH + place * NG + lax.rem(grp + k, NG))
+        c_group(half * NH + place * NG + lax.rem(grp + k, NG), 6)
 
     take(ND - GP, recv.at[4])
-    by_neighbours(lambda a, b: take_c(a + b + a * b, recv.at[2]))
+    by_neighbours(lambda a, b: take_c(a + a * b, recv.at[2]))
+    take_c(GP // 2 - 1, recv.at[9])
     tiles = coarse_vector(rows[0])
     q = as_list(solve(tiles, call[here]))
-    qn = [as_list(solve(tiles, c_in[d])) for d in range(8)]
+    qn = [as_list(solve(tiles, rows_of(d))) for d in range(8)]
 
     def either(hi, lo):
         return [jnp.where(row8 < SUB // 2, a, b) for a, b in zip(hi, lo)]
@@ -955,7 +965,7 @@
     make_row(1, tuple(acc1) + (acc2[ncr],) + tuple(acc2[:ncr]))
     each_peer(lambda t: rows_to(1, 4, t, 3, 7))
 
-    take_c((GP // 2 - 1) * NG, recv.at[6])
+    take_c((GP // 2 - 1) * (NG - 1), recv.at[6])
     swap_half = call.at[pl.ds(half * NH, NH)]
     swap = pltpu.make_async_remote_copy(
         src_ref=swap_half, dst_ref=swap_half, send_sem=send.at[2], recv_sem=recv.at[8],
@@ -963,7 +973,7 @@
     swap.start()
     by_neighbours(lambda a, b: take(
         sum(halo_rows(n, a, b) for n in range(3)) + GP - 1 + (NG - 1) * GP, send.at[0]))
-    by_neighbours(lambda a, b: take_c(a + b + a * b, send.at[1]))
+    by_neighbours(lambda a, b: take_c(a + a * b, send.at[1]))
     swap.wait_recv()
     take(4 * (ND - 1), recv.at[7])
 
@@ -1017,7 +1027,7 @@
         sc_o[n:n + 1, :] = jnp.broadcast_to(v, (1, LANES))
     q_o[0] = jnp.broadcast_to(solve(b1, call[here]), (ncr, LANES))
     for d in range(4):
-        q_o[d + 1] = jnp.broadcast_to(solve(b1, c_in[d]), (ncr, LANES))
+        q_o[d + 1] = jnp.broadcast_to(solve(b1, rows_of(d)), (ncr, LANES))
 
     take(4 * (ND - 1), send.at[3])
     take_c(NG - 1 + (GP // 2 - 1) * NG + NH, send.at[2])
@@ -1088,7 +1098,7 @@
         V(scal, i32), V(scal, i32), V(ext, f32), V(scal, f32), V(scal, f32),
         V((ND, ncr, NC), f32), V((8, ncr, NC), f32), V((X, Z), f32), V((2, X, Z), i32), V((2, ND, LANES), f32),
         V((5, SUB, LANES), f32), V((5, ND, LANES), f32), V((4 * X * Y, LANES), f32),
-        DMA((3,)), DMA((4,)), DMA((9,)),
+        DMA((3,)), DMA((4,)), DMA((10,)),
         pltpu.SemaphoreType.REGULAR((ng - 1,)),
     ]
     outs = (V(ext, f32),) * 3 + (V(field, f32),) * 2 + (V(scal, i32),) + (V(scal, f32),) * 6 + (V((5, ncr, LANES), f32), V((SUB, LANES), f32))

time: 20.3 us -> 20.1 us (level)
    pallas_call x1, Pallas kernels: 18.3 us -> 18.1 us  [local_fast(): pl.pallas_call(functools.partial(kernel, nw, nn), out_shape=outs, in_spec...]
where the time goes in v8:
time: 20.1 us; the launch traced here: 19.9 us
  Pallas kernels  19.3 us (96%)
  between operations  0.64 us (3%)
    pallas_call x1, Pallas kernels, local_fast(): pl.pallas_call(functools.partial(kernel, nw, nn), out_shape=outs, in_spec...  18.1 us
    pallas_call x1, Pallas kernels, local_fast(): pl.pallas_call(finish, out_shape=(jax.ShapeDtypeStruct(field, f32),) * 2,...  1.2 us

profile of v8, /device:TPU:0, one launch (start us, length us, event | category | flops | bytes accessed | tf_op | source)
XLA Modules:
  0.0 19.9 jit_solution(11795086534630058535)
XLA Ops:
  0.6 18.1 %shard_map.59 = (f32[3,22,32,128]{3,2,1,0:T(8,128)S(1)}, f32[3,22,32,128]{3,2,1,0:T(8,128)S(1)}, f32[3,22,32,128]{3,2,1,0:T(8,128)S(1)}, f32[3,16,16,128]{3,2,1,...) custom-call(f32[3,16,16,128]{3,2,1,0:T(8,128)} %r_hbm.1, ...), custom_call_target="tpu_custom_call" | custom-call | tf_op jit(solution)/shard_map/pallas_call | solution.py:1105
  18.7 1.2 %shard_map.60 = (f32[3,16,16,128]{3,2,1,0:T(8,128)}, f32[3,16,16,128]{3,2,1,0:T(8,128)}) custom-call(f32[3,22,32,128]{3,2,1,0:T(8,128)S(1)} %get-tuple-element.16.z_v, f32[3,22,32,128]{3,2,1,0:T(8,128)S(1)} %get-tuple-element.17.g_v, f32[3,22,32,128]{3,2,1,0:T(8,128)S(1)} %get-tuple-element.18.y_v, f32[3,16,16,128]{3,2,1,0:T(8,128)S(1)} %get-tuple-element.19.r_v, ...), custom_call_target="tpu_custom_call" | custom-call | tf_op jit(solution)/shard_map/pallas_call | solution.py:1113

commit v9 on v8

--- a/solution.py
+++ b/solution.py
@@ -490,7 +490,7 @@
 def kernel(nw, nn, r_hbm, occ_hbm, reg_hbm, ci_hbm,
            z_e, g_e, y_e, r_o, ag_o, reg_o, k4, dg, kx, kyp, kzm, kzp, q_o, sc_o,
            occ_e, reg_e, r_e, k_e, invd,
-           call, c_in, y_face, y_label, qpair, row_send, rows, sizes,
+           call, c_in, y_face, y_label, qpair, place_of, row_send, rows, sizes,
            load_sem, send, recv, ready):
     E, YE, Z = occ_e.shape
     X, Y = E - 2 * DEEP, YE - 2 * SUB
@@ -965,6 +965,23 @@
     make_row(1, tuple(acc1) + (acc2[ncr],) + tuple(acc2[:ncr]))
     each_peer(lambda t: rows_to(1, 4, t, 3, 7))
 
+    rr = lax.broadcasted_iota(jnp.int32, (ncr, LANES), 0)
+    ll = lax.broadcasted_iota(jnp.int32, (ncr, LANES), 1)
+    m0, m1 = rr < 0, rr < 0
+    for h in range(G):
+        for g in range(G):
+            for c in range(3):
+                k = (h * G + g) * 3 + c
+                m0 = jnp.logical_or(m0, (ll == k) & (rr == h * 3 + c))
+                m1 = jnp.logical_or(m1, (ll == k) & (rr == g * 3 + c))
+        for c in range(3):
+            for e in range(3):
+                k = 3 * n2 + h * 9 + c * 3 + e
+                m0 = jnp.logical_or(m0, (ll == k) & (rr == h * 3 + c))
+                m1 = jnp.logical_or(m1, (ll == k) & (rr == h * 3 + e))
+    place_of[0] = jnp.where(m0, 1.0, 0.0)
+    place_of[1] = jnp.where(m1, 1.0, 0.0)
+
     take_c((GP // 2 - 1) * (NG - 1), recv.at[6])
     swap_half = call.at[pl.ds(half * NH, NH)]
     swap = pltpu.make_async_remote_copy(
@@ -980,27 +997,13 @@
     block = rows[1]
     b1 = coarse_vector(block)
     h1 = coarse_vector(pltpu.roll(block, LANES - ncr - 4, 1))
-    rr = lax.broadcasted_iota(jnp.int32, (ncr, LANES), 0)
-    ll = lax.broadcasted_iota(jnp.int32, (ncr, LANES), 1)
-    m0, m1 = rr < 0, rr < 0
-    for h in range(G):
-        for g in range(G):
-            for c in range(3):
-                k = (h * G + g) * 3 + c
-                m0 = jnp.logical_or(m0, (ll == k) & (rr == h * 3 + c))
-                m1 = jnp.logical_or(m1, (ll == k) & (rr == g * 3 + c))
-        for c in range(3):
-            for e in range(3):
-                k = 3 * n2 + h * 9 + c * 3 + e
-                m0 = jnp.logical_or(m0, (ll == k) & (rr == h * 3 + c))
-                m1 = jnp.logical_or(m1, (ll == k) & (rr == h * 3 + e))
     lines = [jnp.zeros((ncr, LANES), f32) for _ in b1]
     for w in range(nw):
         for n in range(nn):
             d = w * nn + n
             q1 = solve(b1, call[w % 2 * NH + ((w % GW) // 2 * nn + n) * NG + w // GW])
-            qpair[0, d:d + 1, :] = jnp.sum(jnp.where(m0, q1, 0.0), axis=0, keepdims=True)
-            qpair[1, d:d + 1, :] = jnp.sum(jnp.where(m1, q1, 0.0), axis=0, keepdims=True)
+            qpair[0, d:d + 1, :] = jnp.sum(place_of[0] * q1, axis=0, keepdims=True)
+            qpair[1, d:d + 1, :] = jnp.sum(place_of[1] * q1, axis=0, keepdims=True)
             for t in range(d * ncr // LANES, (d * ncr + ncr - 1) // LANES + 1):
                 lines[t] = jnp.where(ll + LANES * t == rr + d * ncr, q1, lines[t])
     lines = [jnp.sum(v, axis=0, keepdims=True) for v in lines]
@@ -1047,6 +1050,7 @@
         s = spread_over(reg_v[x, own], q_in, G, inside)
         for c in range(3):
             s_e[c, x, own] = s[c]
+        return s
 
     def fill_sides(x):
         s = spread_over(both_sides(reg_v, Y, x), side, G)
@@ -1056,30 +1060,35 @@
             s_e[c, x, rows_from(-some, some)] = s[c][some:SUB]
 
     def fill_own(i, _):
-        fill(i + DEEP, q[0], True)
-        fill_sides(i + DEEP)
+        x = i + DEEP
+        s = fill(x, q[0], True)
+        fill_sides(x)
+        for c in range(3):
+            xb[c, i] = a * z_v[c, x, own] - b * (g_v[c, x, own] + s[c])
         return 0
 
     fill(DEEP - 1, q[1], False)
     fill(DEEP + X, q[2], False)
-    looped(0, X, fill_own, 0)
     faces = (kx, kyp, kzm, kzp, dg, k4)
     parts = 4
     step = X // parts
 
+    def leave(m, src, dst, n):
+        where = (slice(None), pl.ds(n * step, step))
+        pltpu.make_async_copy(src.at[where], dst.at[where], sem.at[m]).start()
+
     def plane(i, _):
-        x = i + DEEP
-        u, w = apply(s_e, faces, x, 0, Y)
-        for c in range(3):
-            xb[c, i] = a * z_v[c, x, own] - b * (g_v[c, x, own] + u[c])
-            rb[c, i] = r_v[c, i] - a * y_v[c, x, own] + b * (ag_v[c, i] + w[c])
-        return 0
-
+        u, w = apply(s_e, faces, i + DEEP, 0, Y)
+        for c in range(3):
+            rb[c, i] = r_v[c, i] - a * y_v[c, i + DEEP, own] + b * (ag_v[c, i] + w[c])
+        return 0
+
+    for n in range(parts):
+        lax.fori_loop(n * step, (n + 1) * step, fill_own, 0, unroll=True)
+        leave(0, xb, x_out, n)
     for n in range(parts):
         lax.fori_loop(n * step, (n + 1) * step, plane, 0, unroll=True)
-        for m, (src, dst) in enumerate(((xb, x_out), (rb, res_out))):
-            where = (slice(None), pl.ds(n * step, step))
-            pltpu.make_async_copy(src.at[where], dst.at[where], sem.at[m]).start()
+        leave(1, rb, res_out, n)
     pltpu.make_async_copy(xb, x_out, sem.at[0]).wait()
     pltpu.make_async_copy(rb, res_out, sem.at[1]).wait()
 
@@ -1096,7 +1105,7 @@
     DMA = pltpu.SemaphoreType.DMA
     scratch = [
         V(scal, i32), V(scal, i32), V(ext, f32), V(scal, f32), V(scal, f32),
-        V((ND, ncr, NC), f32), V((8, ncr, NC), f32), V((X, Z), f32), V((2, X, Z), i32), V((2, ND, LANES), f32),
+        V((ND, ncr, NC), f32), V((8, ncr, NC), f32), V((X, Z), f32), V((2, X, Z), i32), V((2, ND, LANES), f32), V((2, ncr, LANES), f32),
         V((5, SUB, LANES), f32), V((5, ND, LANES), f32), V((4 * X * Y, LANES), f32),
         DMA((3,)), DMA((4,)), DMA((10,)),
         pltpu.SemaphoreType.REGULAR((ng - 1,)),

time: 20.1 us -> 20 us (level)
  no operation moved by 1% of the time
where the time goes in v9:
time: 20 us; the launch traced here: 19.8 us
  Pallas kernels  19.2 us (96%)
  between operations  0.64 us (3%)
    pallas_call x1, Pallas kernels, local_fast(): pl.pallas_call(functools.partial(kernel, nw, nn), out_shape=outs, in_spec...  18 us
    pallas_call x1, Pallas kernels, local_fast(): pl.pallas_call(finish, out_shape=(jax.ShapeDtypeStruct(field, f32),) * 2,...  1.2 us

profile of v9, /device:TPU:0, one launch (start us, length us, event | category | flops | bytes accessed | tf_op | source)
XLA Modules:
  0.0 19.8 jit_solution(14565651921791462120)
XLA Ops:
  0.6 18.0 %shard_map.59 = (f32[3,22,32,128]{3,2,1,0:T(8,128)S(1)}, f32[3,22,32,128]{3,2,1,0:T(8,128)S(1)}, f32[3,22,32,128]{3,2,1,0:T(8,128)S(1)}, f32[3,16,16,128]{3,2,1,...) custom-call(f32[3,16,16,128]{3,2,1,0:T(8,128)} %r_hbm.1, ...), custom_call_target="tpu_custom_call" | custom-call | tf_op jit(solution)/shard_map/pallas_call | solution.py:1114
  18.6 1.2 %shard_map.60 = (f32[3,16,16,128]{3,2,1,0:T(8,128)}, f32[3,16,16,128]{3,2,1,0:T(8,128)}) custom-call(f32[3,22,32,128]{3,2,1,0:T(8,128)S(1)} %get-tuple-element.16.z_v, f32[3,22,32,128]{3,2,1,0:T(8,128)S(1)} %get-tuple-element.17.g_v, f32[3,22,32,128]{3,2,1,0:T(8,128)S(1)} %get-tuple-element.18.y_v, f32[3,16,16,128]{3,2,1,0:T(8,128)S(1)} %get-tuple-element.19.r_v, ...), custom_call_target="tpu_custom_call" | custom-call | tf_op jit(solution)/shard_map/pallas_call | solution.py:1122

commit v10 on v9

--- a/solution.py
+++ b/solution.py
@@ -687,6 +687,17 @@
             def _():
                 halo(n, d).start()
 
+    def c_column(group):
+        pltpu.make_async_remote_copy(
+            src_ref=call.at[here], dst_ref=call.at[here],
+            send_sem=send.at[2], recv_sem=recv.at[5],
+            device_id=column_of(group), device_id_type=MESH).start()
+
+    for k in range(1, NG):
+        @pl.when(grp >= k)
+        def _():
+            c_column(grp - k)
+
     def c_group(block, sem):
         for i in range(1, GP // 2):
             p = lax.rem(place + i, GP // 2)
@@ -701,17 +712,6 @@
             @pl.when(has[d])
             def _():
                 halo_c(d).start()
-
-    def c_column(group):
-        pltpu.make_async_remote_copy(
-            src_ref=call.at[here], dst_ref=call.at[here],
-            send_sem=send.at[2], recv_sem=recv.at[5],
-            device_id=column_of(group), device_id_type=MESH).start()
-
-    for k in range(1, NG):
-        @pl.when(grp >= k)
-        def _():
-            c_column(grp - k)
 
     def stiff_of(o):
         return jnp.where(o < 0, 0.0, soft_stiff + (bone_stiff - soft_stiff) * o.astype(f32))
@@ -817,11 +817,15 @@
 
     sum_acc = lax.fori_loop(0, X, inner, zero_acc(G), unroll=4)
 
+    take_c(NG - 1, recv.at[5])
+    for k in range(1, NG):
+        c_group(half * NH + place * NG + lax.rem(grp + k, NG), 6)
+
     by_neighbours(lambda a, b: take(halo_rows(1, a, b) + halo_rows(2, a, b), recv.at[1]))
 
     def side_rows(i, _):
         x = i + DEEP
-        y_face[pl.ds(i, 1), :] = kyp[x, rows_from(Y - 1, 1), :]
+        y_face[0, pl.ds(i, 1), :] = kyp[x, rows_from(Y - 1, 1), :]
         y_label[0, pl.ds(i, 1), :] = reg_e[x, rows_from(Y - 1, 1), :]
         y_label[1, pl.ds(i, 1), :] = reg_e[x, rows_from(Y, 1), :]
         return 0
@@ -829,7 +833,7 @@
     looped(0, X, side_rows, 0)
     top = DEEP + X - 1
     x_acc = pairs(zero_acc(n2), reg_e[top, inner_rows], ((reg_e[top + 1, inner_rows], kx[top + 1, inner_rows]),))
-    y_acc = pairs(zero_acc(n2), y_label[0], ((y_label[1], y_face[...]),))
+    y_acc = pairs(zero_acc(n2), y_label[0], ((y_label[1], y_face[0]),))
     rim_col = column(tuple(x_acc) + tuple(y_acc) + tuple(sum_acc))
 
     lane = lax.broadcasted_iota(jnp.int32, (n2, LANES), 1)
@@ -881,10 +885,6 @@
 
     def as_list(q):
         return [q[i:i + 1, :] for i in range(ncr)]
-
-    take_c(NG - 1, recv.at[5])
-    for k in range(1, NG):
-        c_group(half * NH + place * NG + lax.rem(grp + k, NG), 6)
 
     take(ND - GP, recv.at[4])
     by_neighbours(lambda a, b: take_c(a + a * b, recv.at[2]))
@@ -1105,8 +1105,8 @@
     DMA = pltpu.SemaphoreType.DMA
     scratch = [
         V(scal, i32), V(scal, i32), V(ext, f32), V(scal, f32), V(scal, f32),
-        V((ND, ncr, NC), f32), V((8, ncr, NC), f32), V((X, Z), f32), V((2, X, Z), i32), V((2, ND, LANES), f32), V((2, ncr, LANES), f32),
-        V((5, SUB, LANES), f32), V((5, ND, LANES), f32), V((4 * X * Y, LANES), f32),
+        V((ND, ncr, NC), f32), V((8, ncr, NC), f32), V((2, X, Z), f32), V((3, X, Z), i32), V((3, ND, LANES), f32), V((2, ncr, LANES), f32),
+        V((5, SUB, LANES), f32), V((6, ND, LANES), f32), V((4 * X * Y, LANES), f32),
         DMA((3,)), DMA((4,)), DMA((10,)),
         pltpu.SemaphoreType.REGULAR((ng - 1,)),
     ]

time: 20 us -> 19.9 us (level)
  no operation moved by 1% of the time
where the time goes in v10:
time: 19.9 us; the launch traced here: 19.7 us
  Pallas kernels  19.1 us (96%)
  between operations  0.64 us (3%)
    pallas_call x1, Pallas kernels, local_fast(): pl.pallas_call(functools.partial(kernel, nw, nn), out_shape=outs, in_spec...  17.9 us
    pallas_call x1, Pallas kernels, local_fast(): pl.pallas_call(finish, out_shape=(jax.ShapeDtypeStruct(field, f32),) * 2,...  1.2 us

profile of v10, /device:TPU:0, one launch (start us, length us, event | category | flops | bytes accessed | tf_op | source)
XLA Modules:
  0.0 19.7 jit_solution(16128538126783998429)
XLA Ops:
  0.6 17.9 %shard_map.59 = (f32[3,22,32,128]{3,2,1,0:T(8,128)S(1)}, f32[3,22,32,128]{3,2,1,0:T(8,128)S(1)}, f32[3,22,32,128]{3,2,1,0:T(8,128)S(1)}, f32[3,16,16,128]{3,2,1,...) custom-call(f32[3,16,16,128]{3,2,1,0:T(8,128)} %r_hbm.1, ...), custom_call_target="tpu_custom_call" | custom-call | tf_op jit(solution)/shard_map/pallas_call | solution.py:1114
  18.5 1.2 %shard_map.60 = (f32[3,16,16,128]{3,2,1,0:T(8,128)}, f32[3,16,16,128]{3,2,1,0:T(8,128)}) custom-call(f32[3,22,32,128]{3,2,1,0:T(8,128)S(1)} %get-tuple-element.16.z_v, f32[3,22,32,128]{3,2,1,0:T(8,128)S(1)} %get-tuple-element.17.g_v, f32[3,22,32,128]{3,2,1,0:T(8,128)S(1)} %get-tuple-element.18.y_v, f32[3,16,16,128]{3,2,1,0:T(8,128)S(1)} %get-tuple-element.19.r_v, ...), custom_call_target="tpu_custom_call" | custom-call | tf_op jit(solution)/shard_map/pallas_call | solution.py:1122
